TPU v7x, 512 devices: a whole 4x8x8 slice. The times are simulated.
512 devices in a mesh: dp: 16 (over z, x_lo), expert: 32 (over x_hi, y, core).
Axes of the slice: x: 4 (x_hi: 2, x_lo: 2; x = x_hi * 2 + x_lo), y: 8, z: 8, core: 2. Of those that a mesh axis runs over, the one named last changes fastest.
Arguments:
- tokens: bfloat16 [1024, 2048], P('expert', 'dp'), may hold values from -6 to 6
- routes: int32 [1024, 8], P('expert'), may hold values from 0 to 127, all different within a row; in each aligned block of 32 rows (0 to 31, 32 to 63, ...) at most 4 rows name the same one
- route_weight: float32 [1024, 8], P('expert'), may hold values from 0.05 to 0.5
- gate_weight: bfloat16 [128, 2048, 768], P('expert', 'dp'), may hold values from -0.125 to 0.125
- up_weight: bfloat16 [128, 2048, 768], P('expert', 'dp'), may hold values from -0.125 to 0.125
- down_weight: bfloat16 [128, 768, 2048], P('expert', None, 'dp'), may hold values from -0.21875 to 0.21875
- trained_down: float32 [128, 768, 2048], P('expert', 'dp'), may hold values from -0.21875 to 0.21875
Outputs:
- mixed: bfloat16 [1024, 2048], P('expert', 'dp')
- synced_down: bfloat16 [128, 768, 2048], P('expert', None, 'dp')
Inputs may be any that keep to these rules, and one draw needn't show every extreme that they name: `routes`: each row names 8 different experts. Among the 32 rows of one device (aligned blocks), no expert is named more than 4 times, a bound that some block reaches.
All inputs are finite; a program needn't handle non-finite values.
Results may differ from a plain program's by a relative error of at most 0.0058.
Values may be sent and summed in bfloat16 or wider, within the bound.
A program may use at most 64 MiB of HBM per device.

v0:
```python
import jax
import jax.numpy as jnp
from jax import lax
from jax.sharding import Mesh
from jax.sharding import PartitionSpec as P

CAP = 4
DP = ("dp_0", "dp_1")


def in_one_piece(arrays, axis, dim, along):
    ends, at = ([], 0)
    for a in arrays[:-1]:
        at += a.shape[along]
        ends.append(at)
    both = jnp.concatenate(arrays, axis=along)
    return tuple(
        jnp.split(lax.psum_scatter(both, axis, scatter_dimension=dim, tiled=True), ends, axis=along)
    )


def whole_of(shard, axes, dim):
    for axis in reversed(axes):
        shard = lax.all_gather(shard, axis, axis=dim, tiled=True)
    return shard


def local(tokens, routes, route_weight, gate_weight, up_weight, down_weight, trained_down):
    tok_rows, width_local = tokens.shape
    expert_local = gate_weight.shape[0]
    groups = lax.axis_size("expert")
    experts_all = expert_local * groups
    capacity = CAP
    narrowed = trained_down.astype(jnp.bfloat16)
    synced_down = lax.all_to_all(narrowed, DP, split_axis=2, concat_axis=1, tiled=True)
    labels = lax.broadcasted_iota(jnp.int32, (1, 1, experts_all), 2)
    chosen = routes[:, :, None] == labels
    counts = jnp.sum(chosen.astype(jnp.int32), axis=1)
    earlier = jnp.cumsum(counts, axis=0) - counts
    weight_expert = jnp.sum(jnp.where(chosen, route_weight[:, :, None], 0.0), axis=1)
    slot_ids = lax.broadcasted_iota(jnp.int32, (1, 1, capacity), 2)
    placed = (counts[:, :, None] == 1) & (earlier[:, :, None] == slot_ids)
    dispatch = placed.astype(jnp.bfloat16).reshape(tok_rows, experts_all * capacity)
    outgoing = jnp.dot(dispatch.T, tokens, preferred_element_type=jnp.float32).astype(jnp.bfloat16)
    outgoing = outgoing.reshape(groups, expert_local, capacity, width_local)
    arrived = lax.all_to_all(outgoing, "expert", split_axis=0, concat_axis=2, tiled=True)
    arrived = arrived.reshape(expert_local, groups * capacity, width_local)
    gate_part = jnp.einsum("erd,edf->erf", arrived, gate_weight, preferred_element_type=jnp.float32)
    up_part = jnp.einsum("erd,edf->erf", arrived, up_weight, preferred_element_type=jnp.float32)
    gate_sum, up_sum = in_one_piece((gate_part, up_part), DP, 2, 0)
    hidden_part = (jax.nn.silu(gate_sum) * up_sum).astype(jnp.bfloat16)
    hidden = whole_of(hidden_part, DP, 2)
    expert_out = jnp.einsum("erf,efd->erd", hidden, down_weight, preferred_element_type=jnp.float32)
    expert_out = expert_out.astype(jnp.bfloat16).reshape(
        1, expert_local, groups * capacity, width_local
    )
    returned = lax.all_to_all(expert_out, "expert", split_axis=2, concat_axis=0, tiled=True)
    returned = returned.reshape(experts_all * capacity, width_local)
    combine = (weight_expert[:, :, None] * placed.astype(jnp.float32)).reshape(
        tok_rows, experts_all * capacity
    )
    mixed = jnp.dot(
        combine,
        returned.astype(jnp.float32),
        precision=lax.Precision.HIGHEST,
        preferred_element_type=jnp.float32,
    )
    mixed = mixed.astype(jnp.bfloat16)
    return (mixed, synced_down)


def solution(mesh):
    torus = Mesh(mesh.devices.reshape(8, 2, mesh.shape["expert"]), ("dp_0", "dp_1", "expert"))
    placed = (
        P("expert", DP),
        P("expert", None),
        P("expert", None),
        P("expert", DP, None),
        P("expert", DP, None),
        P("expert", None, DP),
        P("expert", DP, None),
    )
    return jax.shard_map(
        local,
        mesh=torus,
        in_specs=placed,
        out_specs=(P("expert", DP), P("expert", None, DP)),
        check_vma=False,
    )
```

profile of v0, /device:TPU:1, one launch (start us, length us, event | category | flops | bytes accessed | tf_op | source)
XLA Modules:
  0.0 192.5 jit_solution(4454366995449416110)
XLA Ops:
  7.2 0.0 copy-start
  7.2 0.0 reduce-scatter.2.cloned.1.call-start
  7.2 0.8 copy.45
  8.1 0.1 convert_reduce_fusion
  8.2 0.1 reduce_window_sum.11
  8.2 0.0 copy-start.3
  8.3 0.1 copy.47
  8.3 0.1 copy.46
  8.5 0.1 eq.66
  8.7 0.1 and.21
  8.7 1.0 convolution_convert_fusion.1
  9.7 21.5 %all_to_all.48 = bf16[32,4,4,128]{3,2,1,0:T(4,128)(2,1)S(1)} all-to-all(bf16[32,4,4,128]{3,2,1,0:T(4,128)(2,1)S(1)} %bitcast.35), channel_id=1, replica_groups=mesh['dp_0'=8,'dp_1'=2,'expert'=32] {'expert'}, dimensions={0} | all-to-all | bytes 262144 | tf_op jit(solution)/shard_map/all_to_all | solution.py:46
  31.2 0.0 copy-done
  31.2 0.4 fusion.10
  31.6 0.0 copy-done.3
  31.6 0.4 fusion.9
  32.0 1.9 pad_maximum_fusion
  33.9 3.5 %copy.51 = f32[8,128,768]{1,0,2:T(8,128)} copy(f32[8,128,768]{2,1,0:T(8,128)} %pad_maximum_fusion) | data formatting | bytes 6291456 | tf_op jit(solution)/shard_map/concatenate | solution.py:16
  37.4 0.0 copy-start.2
  37.4 0.0 reduce-scatter.2.cloned.1.call-update
  37.5 1.4 copy-done.2
  38.8 1.0 convert_element_type.26
  39.8 2.9 %copy.55 = bf16[4,48,2048]{1,0,2:T(4,128)(2,1)S(1)} copy(bf16[4,48,2048]{2,1,0:T(8,128)(2,1)} %convert_element_type.26) | data formatting | bytes 1572864 | tf_op jit(solution)/shard_map/convert_element_type | solution.py:34
  42.7 0.0 copy-start.4
  42.7 3.8 %reshape.83 = bf16[16,2,12288]{2,1,0:T(2,128)(2,1)} reshape(bf16[2048,4,48]{2,1,0:T(4,128)(2,1)S(1)} %bitcast.28) | data formatting | bytes 1572864
  46.5 0.0 copy-start.5
  46.5 10.3 %all-to-all-start.2 = ((bf16[16,2,12288]{2,1,0:T(2,128)(2,1)}), bf16[16,2,12288]{2,1,0:T(2,128)(2,1)S(1)}, u32[]{:S(2)}, u32[]{:S(2)}) async-start(bf16[16,2,12288]{2,1,0:T(2,128)(2,1)} %reshape.83), calls=%async_computation.3 | async-start | bytes 1572864 | tf_op jit(solution)/shard_map/all_to_all | solution.py:35
  56.9 0.0 copy-done.4
  56.9 0.1 copy.48
  56.9 69.5 %reduce-scatter.2.cloned.1.call-done = f32[8,128,48]{1,0,2:T(8,128)} async-done(((f32[8,128,768]{1,0,2:T(8,128)}), f32[8,128,48]{1,0,2:T(8,128)}) %reduce-scatter.2.cloned.1.call-update) | async-done | bytes 196624 | tf_op jit(solution)/shard_map/reduce_scatter | solution.py:18
  126.4 1.1 fusion.8
  127.5 4.3 %all_gather.6 = bf16[4,128,96]{1,0,2:T(4,128)(2,1)S(1)} all-gather(bf16[4,128,48]{1,0,2:T(4,128)(2,1)S(1)} %fusion.8), channel_id=1, replica_groups=mesh['dp_0'=8,'dp_1'=2,'expert'=32] {'dp_1'}, dimensions={2}, use_global_device_ids=true | all-gather | bytes 147456 | tf_op jit(solution)/shard_map/all_gather | solution.py:24
  131.8 21.9 %all_gather.7 = bf16[4,128,768]{1,0,2:T(4,128)(2,1)S(1)} all-gather(bf16[4,128,96]{1,0,2:T(4,128)(2,1)S(1)} %all_gather.6), channel_id=1, replica_groups=mesh['dp_0'=8,'dp_1'=2,'expert'=32] {'dp_0'}, dimensions={2}, use_global_device_ids=true | all-gather | bytes 884736 | tf_op jit(solution)/shard_map/all_gather | solution.py:24
  153.7 0.0 copy-done.5
  153.7 0.4 fusion
  154.1 0.7 copy.53
  154.8 0.0 all-to-all-done.2
  154.8 0.0 copy-start.1
  154.8 19.3 %all-to-all-start.1 = ((bf16[1,4,128,128]{3,1,0,2:T(4,128)(2,1)}), bf16[1,4,128,128]{3,1,0,2:T(4,128)(2,1)S(1)}, u32[]{:S(2)}, u32[]{:S(2)}) async-start(bf16[1,4,128,128]{3,1,0,2:T(4,128)(2,1)} %copy.53), calls=%async_computation.2 | async-start | bytes 262144 | tf_op jit(solution)/shard_map/all_to_all | solution.py:57
  174.2 0.1 select_reduce_fusion
  174.3 0.1 copy.49
  174.4 0.0 copy-done.1
  174.4 0.1 fusion.3
  174.5 5.6 %reshape.84 = bf16[2048,4,48]{2,1,0:T(4,128)(2,1)S(1)} reshape(bf16[16,2,12288]{2,1,0:T(2,128)(2,1)} %copy-done.1) | data formatting | bytes 1572864
  180.2 2.3 %copy.56 = bf16[4,16,48,128]{3,2,1,0:T(8,128)(2,1)} copy(bf16[4,16,48,128]{2,0,3,1:T(4,128)(2,1)S(1)} %bitcast.29) | data formatting | bytes 1572864 | tf_op jit(solution)/shard_map/all_to_all | solution.py:35
  182.4 2.2 %all-to-all-done.1 = bf16[1,4,128,128]{3,1,0,2:T(4,128)(2,1)S(1)} async-done(((bf16[1,4,128,128]{3,1,0,2:T(4,128)(2,1)}), bf16[1,4,128,128]{3,1,0,2:T(4,128)(2,1)S(1)}, u32[]{:S(2)}, u32[]{:S(2)}) %all-to-all-start.1) | async-done | bytes 131104 | tf_op jit(solution)/shard_map/all_to_all | solution.py:57
  184.7 0.1 copy.54
  184.7 1.0 convolution_convert_fusion.2
  (5 shorter events, 0.1 us)
Async XLA Ops:
  7.2 24.1 %copy-start = (bf16[4,128,768]{2,1,0:T(8,128)(2,1)S(1)}, bf16[4,128,768]{2,1,0:T(8,128)(2,1)}, u32[]{:S(2)}) copy-start(bf16[4,128,768]{2,1,0:T(8,128)(2,1)} %param.11) | copy-start | bytes 2359300
  7.2 119.2 %reduce-scatter.2.cloned.1.call-start = ((), (), s32[]{:S(2)}) async-start(), calls=%async_computation.4 | async-start | bytes 3342336 | tf_op jit(solution)/shard_map/reduce_scatter | solution.py:18
  8.2 23.4 %copy-start.3 = (bf16[4,128,768]{2,1,0:T(8,128)(2,1)S(1)}, bf16[4,128,768]{2,1,0:T(8,128)(2,1)}, u32[]{:S(2)}) copy-start(bf16[4,128,768]{2,1,0:T(8,128)(2,1)} %param.10) | copy-start | bytes 2359300
  37.4 1.4 copy-start.2
  42.7 14.2 %copy-start.4 = (f32[32,8]{0,1:T(8,128)S(1)}, f32[32,8]{0,1:T(8,128)}, u32[]{:S(2)}) copy-start(f32[32,8]{0,1:T(8,128)} %param.9) | copy-start | bytes 3076
  46.5 107.1 %copy-start.5 = (bf16[4,768,128]{2,1,0:T(8,128)(2,1)S(1)}, bf16[4,768,128]{2,1,0:T(8,128)(2,1)}, u32[]{:S(2)}) copy-start(bf16[4,768,128]{2,1,0:T(8,128)(2,1)} %param.12) | copy-start | bytes 2359300
  46.5 108.3 %all-to-all-start.2 = ((bf16[16,2,12288]{2,1,0:T(2,128)(2,1)}), bf16[16,2,12288]{2,1,0:T(2,128)(2,1)S(1)}, u32[]{:S(2)}, u32[]{:S(2)}) async-start(bf16[16,2,12288]{2,1,0:T(2,128)(2,1)} %reshape.83), calls=%async_computation.3 | async-start | bytes 1572864 | tf_op jit(solution)/shard_map/all_to_all | solution.py:35
  154.8 19.6 %copy-start.1 = (bf16[16,2,12288]{2,1,0:T(2,128)(2,1)}, bf16[16,2,12288]{2,1,0:T(2,128)(2,1)S(1)}, u32[]{:S(2)}) copy-start(bf16[16,2,12288]{2,1,0:T(2,128)(2,1)S(1)} %all-to-all-done.2) | copy-start | bytes 2359300
  154.8 29.8 %all-to-all-start.1 = ((bf16[1,4,128,128]{3,1,0,2:T(4,128)(2,1)}), bf16[1,4,128,128]{3,1,0,2:T(4,128)(2,1)S(1)}, u32[]{:S(2)}, u32[]{:S(2)}) async-start(bf16[1,4,128,128]{3,1,0,2:T(4,128)(2,1)} %copy.53), calls=%async_computation.2 | async-start | bytes 262144 | tf_op jit(solution)/shard_map/all_to_all | solution.py:57
Sparse Core Ops, SparseCore 0:
  37.6 88.7 reduce-scatter.1
where the time goes:
time: 193 us
  waiting for transfers between devices  71.7 us (37%)
  blocking collectives  47.7 us (25%)
  starting transfers between devices  29.6 us (15%)
  local copies, waits for them, and re-layouts  21.8 us (11%)
  between operations  14.2 us (7%)
  other arithmetic  4.43 us (2%)
  matrix products  3.05 us (2%)
    reduce_scatter x1, waiting for transfers between devices, in_one_piece(): lax.psum_scatter(both, axis, scatter_dimension=dim, tiled=True)  69.5 us
    all_gather x2, blocking collectives, whole_of(): shard = lax.all_gather(shard, axis, axis=dim, tiled=True)  26.2 us
    all_to_all x1, blocking collectives, local(): lax.all_to_all(outgoing, 'expert', split_axis=0, concat_axis=2, tiled=True)  21.5 us
    all_to_all x1, starting transfers between devices, local(): lax.all_to_all(expert_out, 'expert', split_axis=2, concat_axis=0, tiled=T...  19.3 us
    unnamed x16, local copies, waits for them, and re-layouts  11.8 us
    all_to_all x1, starting transfers between devices, local(): lax.all_to_all(narrowed, DP, split_axis=2, concat_axis=1, tiled=True)  10.3 us
  transfers between devices with their start and end apart: 3, of which 2 were waited for; matrix products, arithmetic and copies ran while one was open for 9% of the time, Pallas kernels for 0%

commit v1 on v0

v1 whole, which is shorter than its diff:
```python
import functools

import jax
import jax.numpy as jnp
from jax import lax
from jax.experimental import pallas as pl
from jax.experimental.pallas import tpu as pltpu
from jax.sharding import Mesh
from jax.sharding import PartitionSpec as P

DP = ("z", "xl")
BF = jnp.bfloat16
F32 = jnp.float32


def dot(a, b, precision=None):
    return jnp.dot(a, b, preferred_element_type=F32, precision=precision)


def silu(v):
    return v / (1.0 + jnp.exp(-v))


def kernel(
    tokens, routes, route_weight, gate, up, down, trained,
    mixed, synced,
    out_tok, arr, wg, wu, wd, psend, precv, hid, oute, ret, td, td_send,
    load_sem, w_send, w_recv, d_send, d_recv, p_send, p_recv, h_send, h_recv, e_send, e_recv, a_send, a_recv,
):
    z, xl, g = lax.axis_index("z"), lax.axis_index("xl"), lax.axis_index("expert")
    other = 1 - xl
    seat = g * 2 + xl
    rank = z * 2 + xl
    TOK, WIDTH = tokens.shape
    FF = gate.shape[2]

    def at(z_, xl_, g_):
        return dict(device_id={"z": z_, "xl": xl_, "expert": g_}, device_id_type=pl.DeviceIdType.MESH)

    load_td = pltpu.make_async_copy(trained, td, load_sem.at[0])
    load_td.start()
    loads = []
    here = pl.ds(pl.multiple_of(128 * xl, 128), 128)
    for e in range(2):
        for n, (src, dst) in enumerate(((gate, wg), (up, wu))):
            loads.append(pltpu.make_async_copy(src.at[2 * xl + e], dst.at[e, here], load_sem.at[1 + 2 * e + n]))
    for e in range(2):
        loads.append(pltpu.make_async_copy(down.at[2 * xl + e], wd.at[e, :, here], load_sem.at[5 + e]))
    for load in loads:
        load.start()

    barrier = pltpu.get_barrier_semaphore()

    @pl.loop(1, 64)
    def _(i):
        peer = lax.rem(seat + i, 64)
        pl.semaphore_signal(barrier, inc=1, **at(z, lax.rem(peer, 2), lax.div(peer, 2)))

    @pl.loop(1, 8)
    def _(i):
        peer = lax.rem(z + i, 8)
        pl.semaphore_signal(barrier, inc=1, **at(peer, xl, g))
        pl.semaphore_signal(barrier, inc=1, **at(peer, other, g))

    slots = 512
    row = lax.broadcasted_iota(jnp.int32, (TOK, slots), 1)
    chosen = jnp.zeros((TOK, slots), F32)
    weight = jnp.zeros((TOK, slots), F32)
    for k in range(8):
        hit = routes[:, k : k + 1] == lax.shift_right_logical(row, 2)
        chosen = jnp.where(hit, 1.0, chosen)
        weight = jnp.where(hit, route_weight[:, k : k + 1], weight)
    before = lax.broadcasted_iota(jnp.int32, (TOK, TOK), 1) < lax.broadcasted_iota(jnp.int32, (TOK, TOK), 0)
    earlier = dot(jnp.where(before, 1.0, 0.0).astype(BF), chosen.astype(BF))
    slot = lax.bitwise_and(row, 3).astype(F32)
    placed = jnp.where((chosen > 0.5) & (earlier == slot), 1.0, 0.0)
    combine = placed * weight
    outgoing = lax.dot_general(
        placed.astype(BF), tokens[...], (((0,), (0,)), ((), ())), preferred_element_type=F32
    ).astype(BF)
    out_tok[...] = outgoing.reshape(64, 8, WIDTH)
    arr[xl * 32 + g] = out_tok[seat]

    load_td.wait()
    for r in range(16):
        td_send[r] = td[:, :, 128 * r : 128 * r + 128].astype(BF)

    pl.semaphore_wait(barrier, 77)

    @pl.loop(1, 64)
    def _(i):
        peer = lax.rem(seat + i, 64)
        pltpu.make_async_remote_copy(
            out_tok.at[peer], arr.at[xl * 32 + g], d_send, d_recv, **at(z, lax.rem(peer, 2), lax.div(peer, 2))
        ).start()

    sends = []
    for e in range(2):
        for n, (src, dst) in enumerate(((gate, wg), (up, wu))):
            sends.append(pltpu.make_async_remote_copy(
                src.at[2 * other + e], dst.at[e, here], w_send.at[2 * e + n], w_recv.at[2 * e + n], **at(z, other, g)))
    for e in range(2):
        sends.append(pltpu.make_async_remote_copy(
            down.at[2 * other + e], wd.at[e, :, here], w_send.at[4 + e], w_recv.at[4 + e], **at(z, other, g)))
    for send in sends:
        send.start()

    mine = pl.ds(pl.multiple_of(48 * rank, 16), 48)

    def sync_to(z_, xl_):
        return pltpu.make_async_remote_copy(
            td_send.at[z_ * 2 + xl_], synced.at[:, mine], a_send, a_recv, **at(z_, xl_, g))

    own = pltpu.make_async_copy(td_send.at[rank], synced.at[:, mine], load_sem.at[7])
    own.start()

    @pl.loop(1, 8)
    def _(i):
        sync_to(lax.rem(z + i, 8), xl).start()

    def waited(buf, count, sem):
        return pltpu.make_async_copy(buf.at[pl.ds(0, count)], buf.at[pl.ds(0, count)], sem)

    waited(arr, 63, d_recv).wait()
    x = jnp.concatenate([arr[0:32].reshape(256, WIDTH), arr[32:64].reshape(256, WIDTH)], axis=1)
    r0 = lax.broadcasted_iota(jnp.int32, (256, 256), 0)
    r1 = lax.broadcasted_iota(jnp.int32, (256, 256), 1)

    def grouped(r):
        return (lax.bitwise_and(lax.shift_right_logical(r, 2), 31) * 8
                + lax.shift_right_logical(r, 7) * 4 + lax.bitwise_and(r, 3))

    order = jnp.where(grouped(r0) == r1, 1.0, 0.0).astype(BF)
    back = jnp.where(grouped(r1) == r0, 1.0, 0.0).astype(BF)
    x = dot(order, x).astype(BF)

    for e in range(2):
        xe = x[128 * e : 128 * e + 128]
        for n, w in enumerate((wg, wu)):
            loads[2 * e + n].wait()
            sends[2 * e + n].wait_recv()
            psend[e, :, n] = dot(xe, w[e]).astype(BF).reshape(8, 16, FF)
        precv[e, z] = psend[e, z]

        @pl.loop(1, 8)
        def _(i):
            peer = lax.rem(z + i, 8)
            pltpu.make_async_remote_copy(
                psend.at[e, peer], precv.at[e, z], p_send.at[e], p_recv.at[e], **at(peer, xl, g)).start()

    for e in range(2):
        waited(precv.at[e], 7, p_recv.at[e]).wait()
        total = precv[e, 0].astype(F32)
        for s in range(1, 8):
            total = total + precv[e, s].astype(F32)
        hid[e, z] = (silu(total[0]) * total[1]).astype(BF)

        @pl.loop(1, 8)
        def _(i):
            peer = lax.rem(z + i, 8)
            pltpu.make_async_remote_copy(
                hid.at[e, z], hid.at[e, z], h_send.at[e], h_recv.at[e], **at(peer, xl, g)).start()

    sync_to(z, other).start()

    @pl.loop(1, 8)
    def _(i):
        sync_to(lax.rem(z + i, 8), other).start()

    outs = []
    for e in range(2):
        loads[4 + e].wait()
        sends[4 + e].wait_recv()
        waited(hid.at[e], 7, h_recv.at[e]).wait()
        outs.append(dot(hid[e].reshape(128, FF), wd[e]).astype(BF))
    out = dot(back, jnp.concatenate(outs, axis=0)).astype(BF)
    for n in range(2):
        oute[32 * n : 32 * n + 32] = out[:, 128 * n : 128 * n + 128].reshape(32, 8, WIDTH)
    ret[seat] = oute[xl * 32 + g]

    @pl.loop(1, 64)
    def _(i):
        peer = lax.rem(seat + i, 64)
        px, pg = lax.rem(peer, 2), lax.div(peer, 2)
        pltpu.make_async_remote_copy(
            oute.at[px * 32 + pg], ret.at[seat], e_send, e_recv, **at(z, px, pg)).start()

    waited(ret, 63, e_recv).wait()
    mixed[...] = dot(
        combine, ret[...].reshape(slots, WIDTH).astype(F32), precision=lax.Precision.HIGHEST
    ).astype(BF)

    own.wait()
    pltpu.make_async_copy(td_send.at[pl.ds(0, 15)], td_send.at[pl.ds(0, 15)], a_recv).wait()
    pltpu.make_async_copy(td_send.at[pl.ds(0, 15)], td_send.at[pl.ds(0, 15)], a_send).wait()
    waited(out_tok, 63, d_send).wait()
    waited(oute, 63, e_send).wait()
    for e in range(2):
        waited(psend.at[e], 7, p_send.at[e]).wait()
        waited(hid.at[e], 7, h_send.at[e]).wait()
    for send in sends:
        send.wait_send()


def local(tokens, routes, route_weight, gate, up, down, trained):
    V, A = pl.BlockSpec(memory_space=pltpu.VMEM), pl.BlockSpec(memory_space=pl.ANY)
    dma = pltpu.SemaphoreType.DMA
    FF = gate.shape[2]
    return pl.pallas_call(
        kernel,
        out_shape=(
            jax.ShapeDtypeStruct(tokens.shape, BF),
            jax.ShapeDtypeStruct(down.shape, BF),
        ),
        in_specs=[V, V, V, A, A, A, A],
        out_specs=(V, A),
        scratch_shapes=[
            pltpu.VMEM((64, 8, 128), BF),
            pltpu.VMEM((64, 8, 128), BF),
            pltpu.VMEM((2, 256, FF), BF),
            pltpu.VMEM((2, 256, FF), BF),
            pltpu.VMEM((2, FF, 256), BF),
            pltpu.VMEM((2, 8, 2, 16, FF), BF),
            pltpu.VMEM((2, 8, 2, 16, FF), BF),
            pltpu.VMEM((2, 8, 16, FF), BF),
            pltpu.VMEM((64, 8, 128), BF),
            pltpu.VMEM((64, 8, 128), BF),
            pltpu.VMEM(trained.shape, F32),
            pltpu.VMEM((16, 4, 48, 128), BF),
            dma((8,)), dma((6,)), dma((6,)), dma, dma, dma((2,)), dma((2,)), dma((2,)), dma((2,)), dma, dma, dma, dma,
        ],
        compiler_params=pltpu.CompilerParams(collective_id=0, has_side_effects=True),
        name="moe_step",
    )(tokens, routes, route_weight, gate, up, down, trained)


def solution(mesh):
    torus = Mesh(mesh.devices.reshape(8, 2, mesh.shape["expert"]), ("z", "xl", "expert"))
    placed = (
        P("expert", DP),
        P("expert", None),
        P("expert", None),
        P("expert", DP, None),
        P("expert", DP, None),
        P("expert", None, DP),
        P("expert", DP, None),
    )
    return jax.shard_map(
        local,
        mesh=torus,
        in_specs=placed,
        out_specs=(P("expert", DP), P("expert", None, DP)),
        check_vma=False,
    )
```

time: 193 us -> 75.2 us (0.39)
  waiting for transfers between devices: 71.7 us -> 0 us
  Pallas kernels: 0 us -> 68 us
  blocking collectives: 47.7 us -> 0 us
  starting transfers between devices: 29.6 us -> 0 us
  local copies, waits for them, and re-layouts: 21.8 us -> 6.08 us
  between operations: 14.2 us -> 0.64 us
  other arithmetic: 4.43 us -> 0 us
  matrix products: 3.05 us -> 0 us
    reduce_scatter x1 -> x0, waiting for transfers between devices: 69.5 us -> none  [in_one_piece(): lax.psum_scatter(both, axis, scatter_dimension=dim, tiled=True)]
    pallas_call x0 -> x1, Pallas kernels: none -> 68 us  [local(): pl.pallas_call(kernel, out_shape=(jax.ShapeDtypeStruct(tokens.shape, BF),...]
    all_to_all x2 -> x0, starting transfers between devices: 29.6 us -> none  [the longest x1 19.3 us: local(): lax.all_to_all(expert_out, 'expert', split_axis=2, concat_axis=0, tiled=T...]
    all_gather x2 -> x0, blocking collectives: 26.2 us -> none  [whole_of(): shard = lax.all_gather(shard, axis, axis=dim, tiled=True)]
    all_to_all x1 -> x0, blocking collectives: 21.5 us -> none  [local(): lax.all_to_all(outgoing, 'expert', split_axis=0, concat_axis=2, tiled=True)]
    unnamed x16 -> x4, local copies, waits for them, and re-layouts: 11.8 us -> 6.08 us
    concatenate x1 -> x0, local copies, waits for them, and re-layouts: 3.54 us -> none  [in_one_piece(): both = jnp.concatenate(arrays, axis=along)]
    dot_general x5 -> x0, matrix products: 3.05 us -> none  [the longest x1 0.96 us: local(): jnp.dot(combine, returned.astype(jnp.float32), precision=lax.Precision.HI...]
  transfers between devices with their start and end apart: 3 -> 0, of which waited for: 2 -> 0; matrix products, arithmetic and copies ran while one was open for 9% -> 0% of each run, Pallas kernels for 0% -> 0%
where the time goes in v1:
time: 75.2 us; the launch traced here: 74.8 us
  Pallas kernels  68 us (90%)
  local copies, waits for them, and re-layouts  6.08 us (8%)
    pallas_call x1, Pallas kernels, local(): pl.pallas_call(kernel, out_shape=(jax.ShapeDtypeStruct(tokens.shape, BF),...  68 us
    unnamed x4, local copies, waits for them, and re-layouts  6.08 us

profile of v1, /device:TPU:1, one launch (start us, length us, event | category | flops | bytes accessed | tf_op | source)
XLA Modules:
  0.0 74.8 jit_solution(2310023928855308299)
XLA Ops:
  0.6 1.4 %copy.9.routes = s32[32,8]{1,0:T(8,128)} copy(s32[32,8]{0,1:T(8,128)} %param.8) | data formatting | bytes 2048 | tf_op args[1]
  2.0 1.4 %copy.10.route_weight = f32[32,8]{1,0:T(8,128)} copy(f32[32,8]{0,1:T(8,128)} %param.9) | data formatting | bytes 2048 | tf_op args[2]
  3.4 68.0 %moe_step.1 = (bf16[32,128]{1,0:T(8,128)(2,1)}, bf16[4,768,128]{2,1,0:T(8,128)(2,1)}) custom-call(bf16[32,128]{1,0:T(8,128)(2,1)} %tokens.1, s32[32,8]{1,0:T(8,128)} %copy.9.routes, f32[32,8]{1,0:T(8,128)} %copy.10.route_weight, bf16[4,128,768]{2,1,0:T(8,128)(2,1)} %gate.1, bf16[4,128,768]{2,1,0:T(8,128)(2,1)} %up.1, bf16[4,768,128]{2,1,0:T(8,128)(2,1)} %down.1, ...), custom_call_target="tpu_custom_call" | custom-call | tf_op jit(solution)/shard_map/moe_step/pallas_call | solution.py:209
  71.4 1.3 %copy.13 = bf16[32,128]{1,0:T(8,128)(2,1)} copy(bf16[32,128]{1,0:T(8,128)(2,1)} %get-tuple-element.4) | data formatting | bytes 16384
  72.7 2.1 %copy.14 = bf16[4,768,128]{2,1,0:T(8,128)(2,1)} copy(bf16[4,768,128]{2,1,0:T(8,128)(2,1)} %get-tuple-element.5) | data formatting | bytes 1572864

commit v2 on v0

v2 whole, which is shorter than its diff:
```python
import jax
import jax.numpy as jnp
from jax import lax
from jax.experimental import pallas as pl
from jax.experimental.pallas import tpu as pltpu
from jax.sharding import Mesh
from jax.sharding import PartitionSpec as P

DP = ("z", "xl")
BF = jnp.bfloat16
F32 = jnp.float32
CHUNKS = 4
AWAY = sorted(
    ((dy, flip) for dy in range(8) for flip in range(8) if dy or flip),
    key=lambda a: -(min(a[0], 8 - a[0]) + (a[1] >> 2) * 2 * (1 - (a[1] & 1)) + (a[1] & 1)),
)
ZAWAY = (4, 3, 5, 2, 6, 1, 7)
FAR = ZAWAY + (0,)
DIRECT = (3,)
EARLY = 3
ORDER = (0, 1, 10, 2, 11, 20, 3, 12, 21, 30, 13, 22, 31, 23, 32, 33)


def dot(a, b, precision=None):
    return jnp.dot(a, b, preferred_element_type=F32, precision=precision)


def silu(v):
    return v / (1.0 + jnp.exp(-v))


def kernel(
    tokens_hbm, routes_hbm, route_weight_hbm, gate, up, down, trained,
    mixed, synced,
    tokens, routes, route_weight, out_tok, arr, wgu, wd, psend, precv, pagg, hid, oute, ret, td, td_send, td_relay, combine,
    load_sem, w_send, w_recv, d_send, d_recv, p_send, p_recv, h_send, h_recv, e_send, e_recv, a_send, a_recv,
    x_send, x_recv, b_send, b_recv, r_recv, f_recv,
):
    z, xl, g = lax.axis_index("z"), lax.axis_index("xl"), lax.axis_index("expert")
    other = 1 - xl
    seat = g * 2 + xl
    rank = z * 2 + xl
    TOK, WIDTH = tokens.shape
    FF = gate.shape[2]
    PART = FF // 2

    def at(z_, xl_, g_):
        return dict(device_id={"z": z_, "xl": xl_, "expert": g_}, device_id_type=pl.DeviceIdType.MESH)

    def away(dy, flip):
        y = lax.bitwise_and(g + 2 * dy, 14)
        high = lax.bitwise_and(g, 16)
        high = 16 - high if flip & 4 else high
        core = lax.bitwise_and(g, 1)
        core = 1 - core if flip & 2 else core
        return (other if flip & 1 else xl), high + y + core

    def along(dz):
        return lax.bitwise_and(z + dz, 7)

    small = [
        pltpu.make_async_copy(a, b, load_sem.at[n])
        for n, (a, b) in enumerate(((routes_hbm, routes), (route_weight_hbm, route_weight), (tokens_hbm, tokens)))
    ]
    for load in small:
        load.start()

    with jax.named_scope("signals"):
        barrier = pltpu.get_barrier_semaphore()
        for dy, flip in AWAY:
            px, pg = away(dy, flip)
            pl.semaphore_signal(barrier, inc=1, **at(z, px, pg))
        for dz in ZAWAY:
            pl.semaphore_signal(barrier, inc=1, **at(along(dz), xl, g))

    load_td = pltpu.make_async_copy(trained, td, load_sem.at[3])
    load_td.start()
    here = pl.ds(pl.multiple_of(128 * xl, 128), 128)
    loads, sends = [], []
    for c in range(CHUNKS):
        e, half = c // 2, c % 2
        for n, src in enumerate((gate, up)):
            cols = pl.ds(PART * half, PART)
            dst = wgu.at[c, here, pl.ds(PART * n, PART)]
            loads.append(pltpu.make_async_copy(src.at[2 * xl + e, :, cols], dst, load_sem.at[4 + 2 * c + n]))
            sends.append(pltpu.make_async_remote_copy(
                src.at[2 * other + e, :, cols], dst, w_send.at[2 * c + n], w_recv.at[2 * c + n], **at(z, other, g)))
    for e in range(2):
        dst = wd.at[e, :, here]
        loads.append(pltpu.make_async_copy(down.at[2 * xl + e], dst, load_sem.at[12 + e]))
        sends.append(pltpu.make_async_remote_copy(
            down.at[2 * other + e], dst, w_send.at[8 + e], w_recv.at[8 + e], **at(z, other, g)))
    for load in loads:
        load.start()

    with jax.named_scope("routing"):
        for load in small:
            load.wait()
        slots = 512
        row = lax.broadcasted_iota(jnp.int32, (slots, TOK), 0)
        chosen = jnp.zeros((slots, TOK), F32)
        weight = jnp.zeros((slots, TOK), F32)
        for k in range(8):
            hit = routes[k : k + 1, :] == lax.shift_right_logical(row, 2)
            chosen = jnp.where(hit, 1.0, chosen)
            weight = jnp.where(hit, route_weight[k : k + 1, :], weight)
        before = lax.broadcasted_iota(jnp.int32, (TOK, TOK), 0) < lax.broadcasted_iota(jnp.int32, (TOK, TOK), 1)
        earlier = dot(chosen.astype(BF), jnp.where(before, 1.0, 0.0).astype(BF))
        slot = lax.bitwise_and(row, 3).astype(F32)
        placed = jnp.where((chosen > 0.5) & (earlier == slot), 1.0, 0.0)
        combine[...] = placed * weight
        out_tok[...] = dot(placed.astype(BF), tokens[...]).astype(BF).reshape(64, 8, WIDTH)
        arr[xl * 32 + g] = out_tok[seat]

    with jax.named_scope("barrier"):
        pl.semaphore_wait(barrier, 70)

    with jax.named_scope("issue"):
        for dy, flip in AWAY:
            px, pg = away(dy, flip)
            pltpu.make_async_remote_copy(
                out_tok.at[pg * 2 + px], arr.at[xl * 32 + g], d_send, d_recv, **at(z, px, pg)).start()
        for send in sends:
            send.start()

    with jax.named_scope("cast"):
        load_td.wait()
        for r in range(16):
            td_send[r // 2, r % 2] = td[:, :, 128 * r : 128 * r + 128].astype(BF)

    def rows_of(r):
        return pl.ds(pl.multiple_of(48 * r, 16), 48)

    mine, theirs = rows_of(rank), rows_of(z * 2 + other)
    own = [pltpu.make_async_copy(td_send.at[z, xl], synced.at[:, mine], load_sem.at[14])]
    own[0].start()
    for dz in ZAWAY:
        pltpu.make_async_remote_copy(
            td_send.at[along(dz), xl], synced.at[:, mine], a_send, a_recv, **at(along(dz), xl, g)).start()
    across = [
        pltpu.make_async_remote_copy(
            td_send.at[along(dz), other], td_relay.at[along(dz)], x_send.at[n], x_recv.at[n], **at(z, other, g))
        for n, dz in enumerate(FAR)
    ]
    for copy in across:
        copy.start()

    def waited(buf, count, sem):
        return pltpu.make_async_copy(buf.at[pl.ds(0, count)], buf.at[pl.ds(0, count)], sem)

    with jax.named_scope("wait_d"):
        waited(arr, 63, d_recv).wait()
    x = jnp.concatenate([arr[0:32].reshape(256, WIDTH), arr[32:64].reshape(256, WIDTH)], axis=1)
    r0 = lax.broadcasted_iota(jnp.int32, (256, 256), 0)
    r1 = lax.broadcasted_iota(jnp.int32, (256, 256), 1)

    def grouped(r):
        return (lax.bitwise_and(lax.shift_right_logical(r, 2), 31) * 8
                + lax.shift_right_logical(r, 7) * 4 + lax.bitwise_and(r, 3))

    order = jnp.where(grouped(r0) == r1, 1.0, 0.0).astype(BF)
    back = jnp.where(grouped(r1) == r0, 1.0, 0.0).astype(BF)
    x = dot(order, x).astype(BF)

    def push(src, dst, send_sem, recv_sem, dz):
        pltpu.make_async_remote_copy(src, dst, send_sem, recv_sem, **at(along(dz), xl, g)).start()

    def sign(c):
        return 1 if c % 2 == 0 else -1

    def partial(c):
        e = c // 2
        with jax.named_scope(f"wait_w{c}"):
            for n in range(2):
                loads[2 * c + n].wait()
                sends[2 * c + n].wait_recv()
        psend[c] = dot(x[128 * e : 128 * e + 128], wgu[c]).astype(BF).reshape(8, 16, FF)
        push(psend.at[c, along(4)], precv.at[c, 4], p_send.at[c], r_recv.at[c], 2 * sign(c))
        push(psend.at[c, along(3)], precv.at[c, 2], p_send.at[c], r_recv.at[c], 1)
        push(psend.at[c, along(-3)], precv.at[c, 3], p_send.at[c], r_recv.at[c], -1)
        push(psend.at[c, along(1)], precv.at[c, 0], p_send.at[c], p_recv.at[c], 1)
        push(psend.at[c, along(-1)], precv.at[c, 1], p_send.at[c], p_recv.at[c], -1)

    def relayed(c):
        with jax.named_scope(f"wait_r{c}"):
            waited(precv.at[c], 3, r_recv.at[c]).wait()
        ahead = psend[c, along(2)].astype(F32) + precv[c, 2].astype(F32)
        behind = psend[c, along(-2)].astype(F32) + precv[c, 3].astype(F32)
        far = precv[c, 4].astype(F32)
        if sign(c) > 0:
            ahead = ahead + far
        else:
            behind = behind + far
        pagg[c, 0] = ahead.astype(BF)
        pagg[c, 1] = behind.astype(BF)
        push(pagg.at[c, 0], precv.at[c, 5], p_send.at[c], p_recv.at[c], 2)
        push(pagg.at[c, 1], precv.at[c, 6], p_send.at[c], p_recv.at[c], -2)

    def reduced(c):
        with jax.named_scope(f"wait_p{c}"):
            waited(precv.at[c], 4, p_recv.at[c]).wait()
        total = psend[c, z].astype(F32)
        for s in (0, 1, 5, 6):
            total = total + precv[c, s].astype(F32)
        hid[c, z] = (silu(total[:, :PART]) * total[:, PART:]).astype(BF)
        block = hid.at[c, z]
        if c in DIRECT:
            for dz in ZAWAY:
                push(block, block, h_send.at[c], h_recv.at[c], dz)
        else:
            for dz in (2, -2):
                push(block, block, h_send.at[c], f_recv.at[c], dz)
            for dz in (1, -1):
                push(block, block, h_send.at[c], h_recv.at[c], dz)

    def forwarded(c):
        if c in DIRECT:
            return
        with jax.named_scope(f"wait_f{c}"):
            waited(hid.at[c], 2, f_recv.at[c]).wait()
        left, right = hid.at[c, along(-2)], hid.at[c, along(2)]
        if sign(c) > 0:
            push(left, left, h_send.at[c], h_recv.at[c], 2)
        else:
            push(right, right, h_send.at[c], h_recv.at[c], -2)
        push(left, left, h_send.at[c], h_recv.at[c], 1)
        push(right, right, h_send.at[c], h_recv.at[c], -1)

    def hop(n):
        dz = FAR[n]
        with jax.named_scope(f"wait_x{n}"):
            across[n].wait_recv()
        if dz == 0:
            own.append(pltpu.make_async_copy(td_relay.at[z], synced.at[:, theirs], load_sem.at[15]))
            own[1].start()
        else:
            push(td_relay.at[along(dz)], synced.at[:, theirs], b_send, b_recv, dz)

    stages = (partial, relayed, reduced, forwarded)
    for step in ORDER:
        stages[step // 10](step % 10)

    for n in range(EARLY):
        hop(n)
    outs = []
    for e in range(2):
        with jax.named_scope("wait_wd"):
            loads[8 + e].wait()
            sends[8 + e].wait_recv()
        out = None
        for half in range(2):
            c = 2 * e + half
            with jax.named_scope(f"wait_h{c}"):
                waited(hid.at[c], 7 if c in DIRECT else 5, h_recv.at[c]).wait()
            term = dot(hid[c].reshape(128, PART), wd[e, PART * half : PART * half + PART])
            out = term if out is None else out + term
        outs.append(out.astype(BF))
    out = dot(back, jnp.concatenate(outs, axis=0)).astype(BF)
    for n in range(2):
        oute[32 * n : 32 * n + 32] = out[:, 128 * n : 128 * n + 128].reshape(32, 8, WIDTH)
    ret[seat] = oute[xl * 32 + g]
    with jax.named_scope("issue_e"):
        for dy, flip in AWAY:
            px, pg = away(dy, flip)
            pltpu.make_async_remote_copy(
                oute.at[px * 32 + pg], ret.at[seat], e_send, e_recv, **at(z, px, pg)).start()

    for n in range(EARLY, 8):
        hop(n)
    with jax.named_scope("wait_e"):
        waited(ret, 63, e_recv).wait()
    mixed[...] = lax.dot_general(
        combine[...], ret[...].reshape(slots, WIDTH).astype(F32), (((0,), (0,)), ((), ())),
        precision=lax.Precision.HIGHEST, preferred_element_type=F32,
    ).astype(BF)

    with jax.named_scope("wait_a"):
        for copy in own:
            copy.wait()
        for sem in (a_recv, a_send, b_recv, b_send):
            waited(td_relay, 7, sem).wait()
        for copy in across:
            copy.wait_send()

    with jax.named_scope("wait_sends"):
        waited(out_tok, 63, d_send).wait()
        waited(oute, 63, e_send).wait()
        for c in range(CHUNKS):
            waited(psend.at[c], 7, p_send.at[c]).wait()
            waited(hid.at[c], 7, h_send.at[c]).wait()
        for send in sends:
            send.wait_send()


def write_out(mixed, synced, mixed_out, synced_out, sem):
    copies = [
        pltpu.make_async_copy(mixed, mixed_out, sem.at[0]),
        pltpu.make_async_copy(synced, synced_out, sem.at[1]),
    ]
    for copy in copies:
        copy.start()
    for copy in copies:
        copy.wait()


def local(tokens, routes, route_weight, gate, up, down, trained):
    V, A = pl.BlockSpec(memory_space=pltpu.VMEM), pl.BlockSpec(memory_space=pl.ANY)
    dma = pltpu.SemaphoreType.DMA
    FF = gate.shape[2]
    out = pl.pallas_call(
        kernel,
        out_shape=(pltpu.VMEM(tokens.shape, BF), pltpu.VMEM(down.shape, BF)),
        in_specs=[A] * 7,
        out_specs=(V, V),
        scratch_shapes=[
            pltpu.VMEM(tokens.shape, BF),
            pltpu.VMEM((8, 32), jnp.int32),
            pltpu.VMEM((8, 32), F32),
            pltpu.VMEM((64, 8, 128), BF),
            pltpu.VMEM((64, 8, 128), BF),
            pltpu.VMEM((CHUNKS, 256, FF), BF),
            pltpu.VMEM((2, FF, 256), BF),
            pltpu.VMEM((CHUNKS, 8, 16, FF), BF),
            pltpu.VMEM((CHUNKS, 7, 16, FF), BF),
            pltpu.VMEM((CHUNKS, 2, 16, FF), BF),
            pltpu.VMEM((CHUNKS, 8, 16, FF // 2), BF),
            pltpu.VMEM((64, 8, 128), BF),
            pltpu.VMEM((64, 8, 128), BF),
            pltpu.VMEM(trained.shape, F32),
            pltpu.VMEM((8, 2, 4, 48, 128), BF),
            pltpu.VMEM((8, 4, 48, 128), BF),
            pltpu.VMEM((512, 32), F32),
            dma((16,)), dma((10,)), dma((10,)), dma, dma, dma((CHUNKS,)), dma((CHUNKS,)),
            dma((CHUNKS,)), dma((CHUNKS,)), dma, dma, dma, dma, dma((8,)), dma((8,)), dma, dma, dma((CHUNKS,)), dma((CHUNKS,)),
        ],
        compiler_params=pltpu.CompilerParams(collective_id=0, has_side_effects=True),
        name="moe_step",
    )(tokens, routes.T, route_weight.T, gate, up, down, trained)
    out = [pltpu.with_memory_space_constraint(o, pltpu.VMEM) for o in out]
    return pl.pallas_call(
        write_out,
        out_shape=(jax.ShapeDtypeStruct(tokens.shape, BF), jax.ShapeDtypeStruct(down.shape, BF)),
        in_specs=[V, V],
        out_specs=(A, A),
        scratch_shapes=[dma((2,))],
        name="write_out",
    )(*out)


def solution(mesh):
    torus = Mesh(mesh.devices.reshape(8, 2, mesh.shape["expert"]), ("z", "xl", "expert"))
    placed = (
        P("expert", DP),
        P("expert", None),
        P("expert", None),
        P("expert", DP, None),
        P("expert", DP, None),
        P("expert", None, DP),
        P("expert", DP, None),
    )
    return jax.shard_map(
        local,
        mesh=torus,
        in_specs=placed,
        out_specs=(P("expert", DP), P("expert", None, DP)),
        check_vma=False,
    )
```

time: 193 us -> 62.2 us (0.32)
  waiting for transfers between devices: 71.7 us -> 0 us
  Pallas kernels: 0 us -> 61.4 us
  blocking collectives: 47.7 us -> 0 us
  starting transfers between devices: 29.6 us -> 0 us
  local copies, waits for them, and re-layouts: 21.8 us -> 0 us
  between operations: 14.2 us -> 0.64 us
  other arithmetic: 4.43 us -> 0 us
  matrix products: 3.05 us -> 0 us
    reduce_scatter x1 -> x0, waiting for transfers between devices: 69.5 us -> none  [in_one_piece(): lax.psum_scatter(both, axis, scatter_dimension=dim, tiled=True)]
    pallas_call x0 -> x2, Pallas kernels: none -> 61.4 us  [the longest x1 60.5 us: local(): pl.pallas_call(kernel, out_shape=(pltpu.VMEM(tokens.shape, BF), pltpu.VME...]
    all_to_all x2 -> x0, starting transfers between devices: 29.6 us -> none  [the longest x1 19.3 us: local(): lax.all_to_all(expert_out, 'expert', split_axis=2, concat_axis=0, tiled=T...]
    all_gather x2 -> x0, blocking collectives: 26.2 us -> none  [whole_of(): shard = lax.all_gather(shard, axis, axis=dim, tiled=True)]
    all_to_all x1 -> x0, blocking collectives: 21.5 us -> none  [local(): lax.all_to_all(outgoing, 'expert', split_axis=0, concat_axis=2, tiled=True)]
    unnamed x16 -> x0, local copies, waits for them, and re-layouts: 11.8 us -> none
    concatenate x1 -> x0, local copies, waits for them, and re-layouts: 3.54 us -> none  [in_one_piece(): both = jnp.concatenate(arrays, axis=along)]
    dot_general x5 -> x0, matrix products: 3.05 us -> none  [the longest x1 0.96 us: local(): jnp.dot(combine, returned.astype(jnp.float32), precision=lax.Precision.HI...]
  transfers between devices with their start and end apart: 3 -> 0, of which waited for: 2 -> 0; matrix products, arithmetic and copies ran while one was open for 9% -> 0% of each run, Pallas kernels for 0% -> 0%
where the time goes in v2:
time: 62.2 us; the launch traced here: 62.1 us
  Pallas kernels  61.4 us (99%)
  between operations  0.64 us (1%)
    pallas_call x1, Pallas kernels, local(): pl.pallas_call(kernel, out_shape=(pltpu.VMEM(tokens.shape, BF), pltpu.VME...  60.5 us

profile of v2, /device:TPU:1, one launch (start us, length us, event | category | flops | bytes accessed | tf_op | source)
XLA Modules:
  0.0 62.1 jit_solution(14161488934612613168)
XLA Ops:
  0.6 60.5 %moe_step.1 = (bf16[32,128]{1,0:T(8,128)(2,1)S(1)}, bf16[4,768,128]{2,1,0:T(8,128)(2,1)S(1)}) custom-call(bf16[32,128]{1,0:T(8,128)(2,1)} %tokens_hbm.1, s32[8,32]{1,0:T(8,128)} %bitcast.2, f32[8,32]{1,0:T(8,128)} %bitcast.3, bf16[4,128,768]{2,1,0:T(8,128)(2,1)} %gate.1, bf16[4,128,768]{2,1,0:T(8,128)(2,1)} %up.1, bf16[4,768,128]{2,1,0:T(8,128)(2,1)} %down.1, ...), custom_call_target="tpu_custom_call" | custom-call | tf_op jit(solution)/shard_map/moe_step/pallas_call | solution.py:310
  61.2 0.9 %write_out.1 = (bf16[32,128]{1,0:T(8,128)(2,1)}, bf16[4,768,128]{2,1,0:T(8,128)(2,1)}) custom-call(bf16[32,128]{1,0:T(8,128)(2,1)S(1)} %get-tuple-element.4.mixed, bf16[4,768,128]{2,1,0:T(8,128)(2,1)S(1)} %get-tuple-element.5.synced), custom_call_target="tpu_custom_call" | custom-call | tf_op jit(solution)/shard_map/write_out/pallas_call | solution.py:340

commit v3 on v2

v3 whole, which is shorter than its diff:
```python
import jax
import jax.numpy as jnp
from jax import lax
from jax.experimental import pallas as pl
from jax.experimental.pallas import tpu as pltpu
from jax.sharding import Mesh
from jax.sharding import PartitionSpec as P

DP = ("z", "xl")
BF = jnp.bfloat16
F32 = jnp.float32
MESH = pl.DeviceIdType.MESH
PIECES = ((640, 128, 0), (0, 384, 0), (384, 256, 0), (0, 384, 1), (384, 256, 1))
STRAIGHT = ()
DIRECT = (0, 3, 4)
EARLY = 4
SOON = 1
ORDER = (0, 1, 2, 10, 11, 3, 12, 20, 4, 21, 13, 22, 40, 14, 31, 32, 23, 30, 24, 33, 34)
AWAY = sorted(
    ((dy, flip) for dy in range(8) for flip in range(8) if dy or flip),
    key=lambda a: -(min(a[0], 8 - a[0]) + (a[1] >> 2) * 2 * (1 - (a[1] & 1)) + (a[1] & 1)),
)
ZAWAY = (4, 3, 5, 2, 6, 1, 7)
FAR = ZAWAY + (0,)


def dot(a, b, precision=None):
    return jnp.dot(a, b, preferred_element_type=F32, precision=precision)


def silu(v):
    return v / (1.0 + jnp.exp(-v))


def bits(v, shift, mask):
    return lax.bitwise_and(lax.shift_right_logical(v, shift), mask)


def experts_in(n):
    return 4 if n == 0 else 1


def kernel(*refs):
    (tokens_hbm, routes_hbm, route_weight_hbm, gate, up, down, trained, mixed, synced,
     tokens, routes, route_weight, out_tok, arr_s, arr_o, wd, oute, ret, td, td_send, td_relay, combine,
     half_sum, half_send, half_recv) = refs[:25]
    (load_sem, wl_sem, w_send, w_recv, d_send, d_recv, o_recv, p_send, p_recv, r_recv, h_send, h_recv, f_recv,
     e_send, e_recv, a_send, a_recv, b_send, b_recv, x_send, x_recv, half_sem, s_sem) = refs[25:48]
    count = len(PIECES)
    weights, leaving, psend, precv, pagg, hid = (refs[48 + count * i : 48 + count * (i + 1)] for i in range(6))

    z, xl, g = lax.axis_index("z"), lax.axis_index("xl"), lax.axis_index("expert")
    other = 1 - xl
    seat = g * 2 + xl
    rank = z * 2 + xl
    TOK, WIDTH = tokens.shape

    def at(z_, xl_, g_):
        return dict(device_id={"z": z_, "xl": xl_, "expert": g_}, device_id_type=MESH)

    def away(dy, flip):
        y = lax.bitwise_and(g + 2 * dy, 14)
        high = lax.bitwise_and(g, 16)
        high = 16 - high if flip & 4 else high
        core = lax.bitwise_and(g, 1)
        core = 1 - core if flip & 2 else core
        return (other if flip & 1 else xl), high + y + core

    def along(dz):
        return lax.bitwise_and(z + dz, 7)

    small = [
        pltpu.make_async_copy(a, b, load_sem.at[n])
        for n, (a, b) in enumerate(((routes_hbm, routes), (route_weight_hbm, route_weight), (tokens_hbm, tokens)))
    ]
    for load in small:
        load.start()

    with jax.named_scope("signals"):
        barrier = pltpu.get_barrier_semaphore()
        for dy, flip in AWAY:
            px, pg = away(dy, flip)
            pl.semaphore_signal(barrier, inc=1, **at(z, px, pg))
        for dz in ZAWAY:
            pl.semaphore_signal(barrier, inc=1, **at(along(dz), xl, g))

    load_td = pltpu.make_async_copy(trained, td, load_sem.at[3])
    load_td.start()
    loads = [[] for _ in PIECES]
    sends = [[] for _ in PIECES]
    staged = []
    for n, (first, width, e) in enumerate(PIECES):
        for m, src in enumerate((gate, up)):
            cols, into = pl.ds(first, width), pl.ds(width * m, width)
            if n == 0:
                for q in range(4):
                    pair = xl if q < 2 else other
                    loads[0].append(pltpu.make_async_copy(
                        src.at[2 * pair + q % 2, :, cols], weights[0].at[q, :, into], wl_sem.at[4 * m + q]))
            else:
                loads[n].append(pltpu.make_async_copy(
                    src.at[2 * xl + e, :, cols], weights[n].at[0:WIDTH, into], wl_sem.at[6 + 2 * n + m]))
                staged.append(pltpu.make_async_copy(
                    src.at[2 * other + e, :, cols], leaving[n].at[:, into], s_sem.at[2 * n + m]))
                sends[n].append(pltpu.make_async_remote_copy(
                    leaving[n].at[:, into], weights[n].at[WIDTH : 2 * WIDTH, into],
                    w_send.at[2 * n + m], w_recv.at[2 * n + m], **at(z, other, g)))
    down_loads, down_sends, down_staged = [], [], []
    for e in range(2):
        down_loads.append(pltpu.make_async_copy(down.at[2 * xl + e], wd.at[e, :, 0:WIDTH], load_sem.at[4 + e]))
        down_staged.append(pltpu.make_async_copy(down.at[2 * other + e], leaving[0].at[e], s_sem.at[e]))
        down_sends.append(pltpu.make_async_remote_copy(
            leaving[0].at[e], wd.at[e, :, WIDTH : 2 * WIDTH], w_send.at[e], w_recv.at[e], **at(z, other, g)))
    for load in staged + sum(loads, []) + down_staged + down_loads:
        load.start()

    with jax.named_scope("routing"):
        for load in small:
            load.wait()
        slots = 512
        row = lax.broadcasted_iota(jnp.int32, (slots, TOK), 0)
        chosen = jnp.zeros((slots, TOK), F32)
        weight = jnp.zeros((slots, TOK), F32)
        for k in range(8):
            hit = routes[k : k + 1, :] == lax.shift_right_logical(row, 2)
            chosen = jnp.where(hit, 1.0, chosen)
            weight = jnp.where(hit, route_weight[k : k + 1, :], weight)
        before = lax.broadcasted_iota(jnp.int32, (TOK, TOK), 0) < lax.broadcasted_iota(jnp.int32, (TOK, TOK), 1)
        earlier = dot(chosen.astype(BF), jnp.where(before, 1.0, 0.0).astype(BF))
        slot = lax.bitwise_and(row, 3).astype(F32)
        placed = jnp.where((chosen > 0.5) & (earlier == slot), 1.0, 0.0)
        combine[...] = placed * weight
        out_tok[...] = dot(placed.astype(BF), tokens[...]).astype(BF).reshape(64, 8, WIDTH)
        arr_s[2 * g] = out_tok[2 * g]
        arr_s[2 * g + 1] = out_tok[2 * g + 1]

    for copy in staged + down_staged:
        copy.wait()
    with jax.named_scope("barrier"):
        pl.semaphore_wait(barrier, 70)

    with jax.named_scope("issue"):
        for dy, flip in AWAY:
            px, pg = away(dy, flip)
            if flip & 1:
                pltpu.make_async_remote_copy(
                    out_tok.at[pg * 2 + px], arr_o.at[g], d_send, o_recv, **at(z, px, pg)).start()
            else:
                pltpu.make_async_remote_copy(
                    out_tok.at[pl.ds(pg * 2, 2)], arr_s.at[pl.ds(g * 2, 2)], d_send, d_recv, **at(z, px, pg)).start()
        for send in sum(sends, []) + down_sends[:SOON]:
            send.start()

    with jax.named_scope("cast"):
        load_td.wait()
        for r in range(16):
            td_send[r // 2, r % 2] = td[:, :, 128 * r : 128 * r + 128].astype(BF)

    def rows_of(r):
        return pl.ds(pl.multiple_of(48 * r, 16), 48)

    def push(src, dst, send_sem, recv_sem, dz):
        pltpu.make_async_remote_copy(src, dst, send_sem, recv_sem, **at(along(dz), xl, g)).start()

    mine, theirs = rows_of(rank), rows_of(z * 2 + other)
    own = [pltpu.make_async_copy(td_send.at[z, xl], synced.at[:, mine], load_sem.at[6])]
    own[0].start()
    for dz in ZAWAY:
        push(td_send.at[along(dz), xl], synced.at[:, mine], a_send, a_recv, dz)
    across = [
        pltpu.make_async_remote_copy(
            td_send.at[along(dz), other], td_relay.at[along(dz)], x_send.at[n], x_recv.at[n], **at(z, other, g))
        for n, dz in enumerate(FAR)
    ]

    def waited(buf, n, sem):
        return pltpu.make_async_copy(buf.at[pl.ds(0, n)], buf.at[pl.ds(0, n)], sem)

    with jax.named_scope("wait_d"):
        waited(arr_s, 62, d_recv).wait()
        waited(arr_o, 32, o_recv).wait()
    r0 = lax.broadcasted_iota(jnp.int32, (512, 512), 0)
    r1 = lax.broadcasted_iota(jnp.int32, (512, 512), 1)
    pair = lax.bitwise_and(lax.shift_right_logical(r0, 8) + xl, 1)
    source = bits(r0, 2, 31) * 16 + pair * 8 + bits(r0, 7, 1) * 4 + bits(r0, 0, 3)
    x_own = dot(jnp.where(source == r1, 1.0, 0.0).astype(BF), arr_s[...].reshape(512, WIDTH)).astype(BF)

    def grouped(r):
        return bits(r, 2, 31) * 8 + bits(r, 7, 1) * 4 + bits(r, 0, 3)

    r0, r1 = r0[:256, :256], r1[:256, :256]
    order = jnp.where(grouped(r0) == r1, 1.0, 0.0).astype(BF)
    back = jnp.where(grouped(r1) == r0, 1.0, 0.0).astype(BF)
    x_both = jnp.concatenate([x_own[:256], dot(order, arr_o[...].reshape(256, WIDTH)).astype(BF)], axis=1)

    def sign(n):
        return 1 if n % 2 == 0 else -1

    def partial(n):
        width, e = PIECES[n][1:]
        with jax.named_scope(f"wait_w{n}"):
            for copy in loads[n]:
                copy.wait()
            for copy in sends[n]:
                copy.wait_recv()
        if n == 0:
            for q in range(4):
                psend[0][:, q] = dot(x_own[128 * q : 128 * q + 128], weights[0][q]).astype(BF).reshape(8, 16, 2 * width)
        else:
            psend[n][:, 0] = dot(x_both[128 * e : 128 * e + 128], weights[n][...]).astype(BF).reshape(8, 16, 2 * width)
        if n in STRAIGHT:
            for m, dz in enumerate(ZAWAY):
                push(psend[n].at[along(dz)], precv[n].at[m], p_send.at[n], p_recv.at[n], dz)
            return
        push(psend[n].at[along(4)], precv[n].at[4], p_send.at[n], r_recv.at[n], 2 * sign(n))
        push(psend[n].at[along(3)], precv[n].at[2], p_send.at[n], r_recv.at[n], 1)
        push(psend[n].at[along(-3)], precv[n].at[3], p_send.at[n], r_recv.at[n], -1)
        push(psend[n].at[along(1)], precv[n].at[0], p_send.at[n], p_recv.at[n], 1)
        push(psend[n].at[along(-1)], precv[n].at[1], p_send.at[n], p_recv.at[n], -1)

    def relayed(n):
        if n in STRAIGHT:
            return
        with jax.named_scope(f"wait_r{n}"):
            waited(precv[n], 3, r_recv.at[n]).wait()
        ahead = psend[n][along(2)].astype(F32) + precv[n][2].astype(F32)
        behind = psend[n][along(-2)].astype(F32) + precv[n][3].astype(F32)
        far = precv[n][4].astype(F32)
        if sign(n) > 0:
            ahead = ahead + far
        else:
            behind = behind + far
        pagg[n][0] = ahead.astype(BF)
        pagg[n][1] = behind.astype(BF)
        push(pagg[n].at[0], precv[n].at[5], p_send.at[n], p_recv.at[n], 2)
        push(pagg[n].at[1], precv[n].at[6], p_send.at[n], p_recv.at[n], -2)

    def activated(n, total):
        width = PIECES[n][1]
        hid[n][z] = (silu(total[:, :, :width]) * total[:, :, width:]).astype(BF)
        block = hid[n].at[z]
        if n in DIRECT:
            for dz in ZAWAY:
                push(block, block, h_send.at[n], h_recv.at[n], dz)
        else:
            for dz in (2, -2):
                push(block, block, h_send.at[n], f_recv.at[n], dz)
            for dz in (1, -1):
                push(block, block, h_send.at[n], h_recv.at[n], dz)

    halves = pltpu.make_async_remote_copy(half_send, half_recv, half_sem.at[0], half_sem.at[1], **at(z, other, g))

    def reduced(n):
        with jax.named_scope(f"wait_p{n}"):
            waited(precv[n], 7 if n in STRAIGHT else 4, p_recv.at[n]).wait()
        total = psend[n][z].astype(F32)
        for s in range(7) if n in STRAIGHT else (0, 1, 5, 6):
            total = total + precv[n][s].astype(F32)
        if n == 0:
            half_send[...] = total[2:].astype(BF)
            half_sum[...] = total[:2]
            halves.start()
            for copy in down_sends[SOON:] + across:
                copy.start()
        else:
            activated(n, total)

    def both_halves(n):
        with jax.named_scope("wait_half"):
            halves.wait_recv()
        activated(n, half_sum[...] + half_recv[...].astype(F32))

    def forwarded(n):
        if n in DIRECT:
            return
        with jax.named_scope(f"wait_f{n}"):
            waited(hid[n], 2, f_recv.at[n]).wait()
        left, right = hid[n].at[along(-2)], hid[n].at[along(2)]
        if sign(n) > 0:
            push(left, left, h_send.at[n], h_recv.at[n], 2)
        else:
            push(right, right, h_send.at[n], h_recv.at[n], -2)
        push(left, left, h_send.at[n], h_recv.at[n], 1)
        push(right, right, h_send.at[n], h_recv.at[n], -1)

    def hop(n):
        dz = FAR[n]
        with jax.named_scope(f"wait_x{n}"):
            across[n].wait_recv()
        if dz == 0:
            own.append(pltpu.make_async_copy(td_relay.at[z], synced.at[:, theirs], load_sem.at[7]))
            own[1].start()
        else:
            push(td_relay.at[along(dz)], synced.at[:, theirs], b_send, b_recv, dz)

    stages = (partial, relayed, reduced, forwarded, both_halves)
    for step in ORDER:
        stages[step // 10](step % 10)

    for n in range(EARLY):
        hop(n)
    with jax.named_scope("wait_wd"):
        for e in range(2):
            down_loads[e].wait()
            down_sends[e].wait_recv()
    outs = [None, None]
    for n, (first, width, expert) in enumerate(PIECES):
        with jax.named_scope(f"wait_h{n}"):
            waited(hid[n], 7 if n in DIRECT else 5, h_recv.at[n]).wait()
        for m, e in enumerate((0, 1) if n == 0 else (expert,)):
            term = dot(hid[n][:, m].reshape(128, width), wd[e, first : first + width])
            outs[e] = term if outs[e] is None else outs[e] + term
    out = dot(back, jnp.concatenate(outs, axis=0).astype(BF)).astype(BF)
    for n in range(2):
        oute[32 * n : 32 * n + 32] = out[:, WIDTH * n : WIDTH * n + WIDTH].reshape(32, 8, WIDTH)
    ret[seat] = oute[g]
    with jax.named_scope("issue_e"):
        for dy, flip in AWAY:
            px, pg = away(dy, flip)
            pltpu.make_async_remote_copy(
                oute.at[(flip & 1) * 32 + pg], ret.at[seat], e_send, e_recv, **at(z, px, pg)).start()

    for n in range(EARLY, 8):
        hop(n)
    with jax.named_scope("wait_e"):
        waited(ret, 63, e_recv).wait()
    mixed[...] = lax.dot_general(
        combine[...], ret[...].reshape(slots, WIDTH).astype(F32), (((0,), (0,)), ((), ())),
        precision=lax.Precision.HIGHEST, preferred_element_type=F32,
    ).astype(BF)

    with jax.named_scope("wait_a"):
        for copy in own:
            copy.wait()
        for sem in (a_recv, a_send, b_recv, b_send):
            waited(td_relay, 7, sem).wait()
        for copy in across:
            copy.wait_send()
    with jax.named_scope("wait_sends"):
        waited(out_tok, 62, d_send).wait()
        waited(out_tok, 32, d_send).wait()
        waited(oute, 63, e_send).wait()
        halves.wait_send()
        for n in range(count):
            waited(psend[n], 7, p_send.at[n]).wait()
            waited(hid[n], 7, h_send.at[n]).wait()
        for send in sum(sends, []) + down_sends:
            send.wait_send()


def write_out(mixed, synced, mixed_out, synced_out, sem):
    copies = [
        pltpu.make_async_copy(synced, synced_out, sem.at[1]),
        pltpu.make_async_copy(mixed, mixed_out, sem.at[0]),
    ]
    for copy in copies:
        copy.start()
    for copy in copies:
        copy.wait()


def local(tokens, routes, route_weight, gate, up, down, trained):
    V, A = pl.BlockSpec(memory_space=pltpu.VMEM), pl.BlockSpec(memory_space=pl.ANY)
    FF = gate.shape[2]
    count = len(PIECES)
    wide = [2 * width for _, width, _ in PIECES]

    def vmem(*shape, dtype=BF):
        return pltpu.VMEM(shape, dtype)

    def dma(*shape):
        return pltpu.SemaphoreType.DMA(shape)

    scratch = [
        vmem(*tokens.shape), vmem(8, 32, dtype=jnp.int32), vmem(8, 32, dtype=F32),
        vmem(64, 8, 128), vmem(64, 8, 128), vmem(32, 8, 128), vmem(2, FF, 256), vmem(64, 8, 128), vmem(64, 8, 128),
        vmem(*trained.shape, dtype=F32), vmem(8, 2, 4, 48, 128), vmem(8, 4, 48, 128), vmem(512, 32, dtype=F32),
        vmem(2, 16, wide[0], dtype=F32), vmem(2, 16, wide[0]), vmem(2, 16, wide[0]),
        dma(8), dma(8 + 2 * count), dma(2 * count), dma(2 * count), dma(), dma(), dma(),
        dma(count), dma(count), dma(count), dma(count), dma(count), dma(count),
        dma(), dma(), dma(), dma(), dma(), dma(), dma(8), dma(8), dma(2), dma(2 * count),
    ]
    scratch += [vmem(*((4, 128, wide[0]) if n == 0 else (256, wide[n]))) for n in range(count)]
    scratch += [vmem(*((2, FF, 128) if n == 0 else (128, wide[n]))) for n in range(count)]
    for devices in (8, 7, 2):
        scratch += [vmem(devices, experts_in(n), 16, wide[n]) for n in range(count)]
    scratch += [vmem(8, 2 if n == 0 else 1, 16, wide[n] // 2) for n in range(count)]
    out = pl.pallas_call(
        kernel,
        out_shape=(pltpu.VMEM(tokens.shape, BF), pltpu.VMEM(down.shape, BF)),
        in_specs=[A] * 7,
        out_specs=(V, V),
        scratch_shapes=scratch,
        compiler_params=pltpu.CompilerParams(collective_id=0, has_side_effects=True),
        name="moe_step",
    )(tokens, routes.T, route_weight.T, gate, up, down, trained)
    out = [pltpu.with_memory_space_constraint(o, pltpu.VMEM) for o in out]
    return pl.pallas_call(
        write_out,
        out_shape=(jax.ShapeDtypeStruct(tokens.shape, BF), jax.ShapeDtypeStruct(down.shape, BF)),
        in_specs=[V, V],
        out_specs=(A, A),
        scratch_shapes=[dma(2)],
        name="write_out",
    )(*out)


def solution(mesh):
    torus = Mesh(mesh.devices.reshape(8, 2, mesh.shape["expert"]), ("z", "xl", "expert"))
    placed = (
        P("expert", DP),
        P("expert", None),
        P("expert", None),
        P("expert", DP, None),
        P("expert", DP, None),
        P("expert", None, DP),
        P("expert", DP, None),
    )
    return jax.shard_map(
        local,
        mesh=torus,
        in_specs=placed,
        out_specs=(P("expert", DP), P("expert", None, DP)),
        check_vma=False,
    )
```

time: 62.2 us -> 60.5 us (0.973)
  Pallas kernels: 61.4 us -> 59.7 us
    pallas_call x1, Pallas kernels: 60.5 us -> 58.8 us  [local(): pl.pallas_call(kernel, out_shape=(pltpu.VMEM(tokens.shape, BF), pltpu.VME...]
where the time goes in v3:
time: 60.5 us; the launch traced here: 60.3 us
  Pallas kernels  59.7 us (99%)
  between operations  0.64 us (1%)
    pallas_call x1, Pallas kernels, local(): pl.pallas_call(kernel, out_shape=(pltpu.VMEM(tokens.shape, BF), pltpu.VME...  58.8 us

profile of v3, /device:TPU:1, one launch (start us, length us, event | category | flops | bytes accessed | tf_op | source)
XLA Modules:
  0.0 60.3 jit_solution(11135557121221247824)
XLA Ops:
  0.6 58.8 %moe_step.1 = (bf16[32,128]{1,0:T(8,128)(2,1)S(1)}, bf16[4,768,128]{2,1,0:T(8,128)(2,1)S(1)}) custom-call(bf16[32,128]{1,0:T(8,128)(2,1)} %refs_0_.1, s32[8,32]{1,0:T(8,128)} %bitcast.2, f32[8,32]{1,0:T(8,128)} %bitcast.3, bf16[4,128,768]{2,1,0:T(8,128)(2,1)} %refs_3_.1, bf16[4,128,768]{2,1,0:T(8,128)(2,1)} %refs_4_.1, bf16[4,768,128]{2,1,0:T(8,128)(2,1)} %refs_5_.1, ...), custom_call_target="tpu_custom_call" | custom-call | tf_op jit(solution)/shard_map/moe_step/pallas_call | solution.py:388
  59.4 0.9 %write_out.1 = (bf16[32,128]{1,0:T(8,128)(2,1)}, bf16[4,768,128]{2,1,0:T(8,128)(2,1)}) custom-call(bf16[32,128]{1,0:T(8,128)(2,1)S(1)} %get-tuple-element.4.mixed, bf16[4,768,128]{2,1,0:T(8,128)(2,1)S(1)} %get-tuple-element.5.synced), custom_call_target="tpu_custom_call" | custom-call | tf_op jit(solution)/shard_map/write_out/pallas_call | solution.py:398

commit v4 on v3

--- a/solution.py
+++ b/solution.py
@@ -12,8 +12,8 @@
 MESH = pl.DeviceIdType.MESH
 PIECES = ((640, 128, 0), (0, 384, 0), (384, 256, 0), (0, 384, 1), (384, 256, 1))
 STRAIGHT = ()
-DIRECT = (0, 3, 4)
-EARLY = 4
+DIRECT = (3, 4)
+EARLY = 2
 SOON = 1
 ORDER = (0, 1, 2, 10, 11, 3, 12, 20, 4, 21, 13, 22, 40, 14, 31, 32, 23, 30, 24, 33, 34)
 AWAY = sorted(
@@ -41,18 +41,19 @@
 
 
 def kernel(*refs):
-    (tokens_hbm, routes_hbm, route_weight_hbm, gate, up, down, trained, mixed, synced,
-     tokens, routes, route_weight, out_tok, arr_s, arr_o, wd, oute, ret, td, td_send, td_relay, combine,
-     half_sum, half_send, half_recv) = refs[:25]
-    (load_sem, wl_sem, w_send, w_recv, d_send, d_recv, o_recv, p_send, p_recv, r_recv, h_send, h_recv, f_recv,
-     e_send, e_recv, a_send, a_recv, b_send, b_recv, x_send, x_recv, half_sem, s_sem) = refs[25:48]
+    (tokens_hbm, routes_hbm, route_weight_hbm, gate, up, down, trained, ret, shares, synced,
+     tokens, routes, route_weight, out_tok, arr_s, arr_o, wd, oute, td, td_send, td_relay, td_far, combine,
+     half_sum, half_send, half_recv) = refs[:26]
+    (load_sem, wl_sem, sent, w_recv, d_recv, o_recv, p_recv, r_recv, h_recv, f_recv,
+     e_recv, a_recv, b_recv, x_recv, half_sem, s_sem, v_recv) = refs[26:43]
     count = len(PIECES)
-    weights, leaving, psend, precv, pagg, hid = (refs[48 + count * i : 48 + count * (i + 1)] for i in range(6))
+    weights, leaving, psend, precv, pagg, hid = (refs[43 + count * i : 43 + count * (i + 1)] for i in range(6))
 
     z, xl, g = lax.axis_index("z"), lax.axis_index("xl"), lax.axis_index("expert")
     other = 1 - xl
     seat = g * 2 + xl
     rank = z * 2 + xl
+    core = lax.bitwise_and(g, 1)
     TOK, WIDTH = tokens.shape
 
     def at(z_, xl_, g_):
@@ -62,9 +63,8 @@
         y = lax.bitwise_and(g + 2 * dy, 14)
         high = lax.bitwise_and(g, 16)
         high = 16 - high if flip & 4 else high
-        core = lax.bitwise_and(g, 1)
-        core = 1 - core if flip & 2 else core
-        return (other if flip & 1 else xl), high + y + core
+        side = 1 - core if flip & 2 else core
+        return (other if flip & 1 else xl), high + y + side
 
     def along(dz):
         return lax.bitwise_and(z + dz, 7)
@@ -101,16 +101,16 @@
                 loads[n].append(pltpu.make_async_copy(
                     src.at[2 * xl + e, :, cols], weights[n].at[0:WIDTH, into], wl_sem.at[6 + 2 * n + m]))
                 staged.append(pltpu.make_async_copy(
-                    src.at[2 * other + e, :, cols], leaving[n].at[:, into], s_sem.at[2 * n + m]))
+                    src.at[2 * other + e, :, cols], leaving[n].at[:, into], s_sem))
                 sends[n].append(pltpu.make_async_remote_copy(
                     leaving[n].at[:, into], weights[n].at[WIDTH : 2 * WIDTH, into],
-                    w_send.at[2 * n + m], w_recv.at[2 * n + m], **at(z, other, g)))
+                    sent, w_recv.at[2 * n + m], **at(z, other, g)))
     down_loads, down_sends, down_staged = [], [], []
     for e in range(2):
         down_loads.append(pltpu.make_async_copy(down.at[2 * xl + e], wd.at[e, :, 0:WIDTH], load_sem.at[4 + e]))
-        down_staged.append(pltpu.make_async_copy(down.at[2 * other + e], leaving[0].at[e], s_sem.at[e]))
+        down_staged.append(pltpu.make_async_copy(down.at[2 * other + e], leaving[0].at[e], s_sem))
         down_sends.append(pltpu.make_async_remote_copy(
-            leaving[0].at[e], wd.at[e, :, WIDTH : 2 * WIDTH], w_send.at[e], w_recv.at[e], **at(z, other, g)))
+            leaving[0].at[e], wd.at[e, :, WIDTH : 2 * WIDTH], sent, w_recv.at[e], **at(z, other, g)))
     for load in staged + sum(loads, []) + down_staged + down_loads:
         load.start()
 
@@ -144,10 +144,10 @@
             px, pg = away(dy, flip)
             if flip & 1:
                 pltpu.make_async_remote_copy(
-                    out_tok.at[pg * 2 + px], arr_o.at[g], d_send, o_recv, **at(z, px, pg)).start()
+                    out_tok.at[pg * 2 + px], arr_o.at[g], sent, o_recv, **at(z, px, pg)).start()
             else:
                 pltpu.make_async_remote_copy(
-                    out_tok.at[pl.ds(pg * 2, 2)], arr_s.at[pl.ds(g * 2, 2)], d_send, d_recv, **at(z, px, pg)).start()
+                    out_tok.at[pl.ds(pg * 2, 2)], arr_s.at[pl.ds(g * 2, 2)], sent, d_recv, **at(z, px, pg)).start()
         for send in sum(sends, []) + down_sends[:SOON]:
             send.start()
 
@@ -163,19 +163,39 @@
         pltpu.make_async_remote_copy(src, dst, send_sem, recv_sem, **at(along(dz), xl, g)).start()
 
     mine, theirs = rows_of(rank), rows_of(z * 2 + other)
-    own = [pltpu.make_async_copy(td_send.at[z, xl], synced.at[:, mine], load_sem.at[6])]
-    own[0].start()
+    own = [
+        pltpu.make_async_copy(td_send.at[z, xl], synced.at[:, mine], load_sem.at[6]),
+        pltpu.make_async_copy(combine, shares, load_sem.at[8]),
+    ]
+    for copy in own:
+        copy.start()
+
+    def spread(block, rows, far, send_sem, recv_sem, dz):
+        if dz == 4:
+            for way in range(2):
+                push(block.at[pl.ds(2 * way, 2)], td_far.at[far, way], send_sem, v_recv.at[far], 2 - 4 * way)
+        else:
+            push(block, synced.at[:, rows], send_sem, recv_sem, dz)
+
+    def passed_on(far, side, send_sem, recv_sem):
+        with jax.named_scope(f"wait_v{far}"):
+            waited(td_far.at[far], 2, v_recv.at[far]).wait()
+        for way in range(2):
+            dz = 2 - 4 * way
+            push(td_far.at[far, way], synced.at[pl.ds(2 * way, 2), rows_of(along(-dz) * 2 + side)], send_sem, recv_sem, dz)
+
     for dz in ZAWAY:
-        push(td_send.at[along(dz), xl], synced.at[:, mine], a_send, a_recv, dz)
+        spread(td_send.at[along(dz), xl], mine, 0, sent, a_recv, dz)
     across = [
         pltpu.make_async_remote_copy(
-            td_send.at[along(dz), other], td_relay.at[along(dz)], x_send.at[n], x_recv.at[n], **at(z, other, g))
+            td_send.at[along(dz), other], td_relay.at[along(dz)], sent, x_recv.at[n], **at(z, other, g))
         for n, dz in enumerate(FAR)
     ]
 
     def waited(buf, n, sem):
         return pltpu.make_async_copy(buf.at[pl.ds(0, n)], buf.at[pl.ds(0, n)], sem)
 
+    passed_on(0, xl, sent, a_recv)
     with jax.named_scope("wait_d"):
         waited(arr_s, 62, d_recv).wait()
         waited(arr_o, 32, o_recv).wait()
@@ -210,13 +230,13 @@
             psend[n][:, 0] = dot(x_both[128 * e : 128 * e + 128], weights[n][...]).astype(BF).reshape(8, 16, 2 * width)
         if n in STRAIGHT:
             for m, dz in enumerate(ZAWAY):
-                push(psend[n].at[along(dz)], precv[n].at[m], p_send.at[n], p_recv.at[n], dz)
+                push(psend[n].at[along(dz)], precv[n].at[m], sent, p_recv.at[n], dz)
             return
-        push(psend[n].at[along(4)], precv[n].at[4], p_send.at[n], r_recv.at[n], 2 * sign(n))
-        push(psend[n].at[along(3)], precv[n].at[2], p_send.at[n], r_recv.at[n], 1)
-        push(psend[n].at[along(-3)], precv[n].at[3], p_send.at[n], r_recv.at[n], -1)
-        push(psend[n].at[along(1)], precv[n].at[0], p_send.at[n], p_recv.at[n], 1)
-        push(psend[n].at[along(-1)], precv[n].at[1], p_send.at[n], p_recv.at[n], -1)
+        push(psend[n].at[along(4)], precv[n].at[4], sent, r_recv.at[n], 2 * sign(n))
+        push(psend[n].at[along(3)], precv[n].at[2], sent, r_recv.at[n], 1)
+        push(psend[n].at[along(-3)], precv[n].at[3], sent, r_recv.at[n], -1)
+        push(psend[n].at[along(1)], precv[n].at[0], sent, p_recv.at[n], 1)
+        push(psend[n].at[along(-1)], precv[n].at[1], sent, p_recv.at[n], -1)
 
     def relayed(n):
         if n in STRAIGHT:
@@ -232,8 +252,8 @@
             behind = behind + far
         pagg[n][0] = ahead.astype(BF)
         pagg[n][1] = behind.astype(BF)
-        push(pagg[n].at[0], precv[n].at[5], p_send.at[n], p_recv.at[n], 2)
-        push(pagg[n].at[1], precv[n].at[6], p_send.at[n], p_recv.at[n], -2)
+        push(pagg[n].at[0], precv[n].at[5], sent, p_recv.at[n], 2)
+        push(pagg[n].at[1], precv[n].at[6], sent, p_recv.at[n], -2)
 
     def activated(n, total):
         width = PIECES[n][1]
@@ -241,14 +261,14 @@
         block = hid[n].at[z]
         if n in DIRECT:
             for dz in ZAWAY:
-                push(block, block, h_send.at[n], h_recv.at[n], dz)
+                push(block, block, sent, h_recv.at[n], dz)
         else:
             for dz in (2, -2):
-                push(block, block, h_send.at[n], f_recv.at[n], dz)
+                push(block, block, sent, f_recv.at[n], dz)
             for dz in (1, -1):
-                push(block, block, h_send.at[n], h_recv.at[n], dz)
-
-    halves = pltpu.make_async_remote_copy(half_send, half_recv, half_sem.at[0], half_sem.at[1], **at(z, other, g))
+                push(block, block, sent, h_recv.at[n], dz)
+
+    halves = pltpu.make_async_remote_copy(half_send, half_recv, sent, half_sem, **at(z, other, g))
 
     def reduced(n):
         with jax.named_scope(f"wait_p{n}"):
@@ -277,11 +297,11 @@
             waited(hid[n], 2, f_recv.at[n]).wait()
         left, right = hid[n].at[along(-2)], hid[n].at[along(2)]
         if sign(n) > 0:
-            push(left, left, h_send.at[n], h_recv.at[n], 2)
-        else:
-            push(right, right, h_send.at[n], h_recv.at[n], -2)
-        push(left, left, h_send.at[n], h_recv.at[n], 1)
-        push(right, right, h_send.at[n], h_recv.at[n], -1)
+            push(left, left, sent, h_recv.at[n], 2)
+        else:
+            push(right, right, sent, h_recv.at[n], -2)
+        push(left, left, sent, h_recv.at[n], 1)
+        push(right, right, sent, h_recv.at[n], -1)
 
     def hop(n):
         dz = FAR[n]
@@ -289,9 +309,9 @@
             across[n].wait_recv()
         if dz == 0:
             own.append(pltpu.make_async_copy(td_relay.at[z], synced.at[:, theirs], load_sem.at[7]))
-            own[1].start()
-        else:
-            push(td_relay.at[along(dz)], synced.at[:, theirs], b_send, b_recv, dz)
+            own[-1].start()
+        else:
+            spread(td_relay.at[along(dz)], theirs, 1, sent, b_recv, dz)
 
     stages = (partial, relayed, reduced, forwarded, both_halves)
     for step in ORDER:
@@ -313,50 +333,52 @@
     out = dot(back, jnp.concatenate(outs, axis=0).astype(BF)).astype(BF)
     for n in range(2):
         oute[32 * n : 32 * n + 32] = out[:, WIDTH * n : WIDTH * n + WIDTH].reshape(32, 8, WIDTH)
-    ret[seat] = oute[g]
+    own.append(pltpu.make_async_copy(oute.at[g], ret.at[seat], load_sem.at[9]))
+    own[-1].start()
     with jax.named_scope("issue_e"):
         for dy, flip in AWAY:
             px, pg = away(dy, flip)
             pltpu.make_async_remote_copy(
-                oute.at[(flip & 1) * 32 + pg], ret.at[seat], e_send, e_recv, **at(z, px, pg)).start()
+                oute.at[(flip & 1) * 32 + pg], ret.at[seat], sent, e_recv, **at(z, px, pg)).start()
 
     for n in range(EARLY, 8):
         hop(n)
+    passed_on(1, other, sent, b_recv)
     with jax.named_scope("wait_e"):
-        waited(ret, 63, e_recv).wait()
-    mixed[...] = lax.dot_general(
-        combine[...], ret[...].reshape(slots, WIDTH).astype(F32), (((0,), (0,)), ((), ())),
-        precision=lax.Precision.HIGHEST, preferred_element_type=F32,
-    ).astype(BF)
+        waited(oute, 63, e_recv).wait()
 
     with jax.named_scope("wait_a"):
         for copy in own:
             copy.wait()
-        for sem in (a_recv, a_send, b_recv, b_send):
+        for sem in (a_recv, b_recv):
             waited(td_relay, 7, sem).wait()
+        for sem in (sent, sent):
+            waited(td_relay, 8, sem).wait()
         for copy in across:
             copy.wait_send()
     with jax.named_scope("wait_sends"):
-        waited(out_tok, 62, d_send).wait()
-        waited(out_tok, 32, d_send).wait()
-        waited(oute, 63, e_send).wait()
+        waited(out_tok, 62, sent).wait()
+        waited(out_tok, 32, sent).wait()
+        waited(oute, 63, sent).wait()
         halves.wait_send()
         for n in range(count):
-            waited(psend[n], 7, p_send.at[n]).wait()
-            waited(hid[n], 7, h_send.at[n]).wait()
+            waited(psend[n], 7, sent).wait()
+            waited(hid[n], 7, sent).wait()
         for send in sum(sends, []) + down_sends:
             send.wait_send()
 
 
-def write_out(mixed, synced, mixed_out, synced_out, sem):
-    copies = [
-        pltpu.make_async_copy(synced, synced_out, sem.at[1]),
-        pltpu.make_async_copy(mixed, mixed_out, sem.at[0]),
-    ]
-    for copy in copies:
-        copy.start()
-    for copy in copies:
-        copy.wait()
+def write_out(ret, shares, synced, mixed_out, synced_out, mixed, sem):
+    copy = pltpu.make_async_copy(synced, synced_out, sem.at[1])
+    copy.start()
+    mixed[...] = lax.dot_general(
+        shares[...], ret[...].reshape(shares.shape[0], ret.shape[2]).astype(F32), (((0,), (0,)), ((), ())),
+        precision=lax.Precision.HIGHEST, preferred_element_type=F32,
+    ).astype(BF)
+    last = pltpu.make_async_copy(mixed, mixed_out, sem.at[0])
+    last.start()
+    copy.wait()
+    last.wait()
 
 
 def local(tokens, routes, route_weight, gate, up, down, trained):
@@ -373,12 +395,12 @@
 
     scratch = [
         vmem(*tokens.shape), vmem(8, 32, dtype=jnp.int32), vmem(8, 32, dtype=F32),
-        vmem(64, 8, 128), vmem(64, 8, 128), vmem(32, 8, 128), vmem(2, FF, 256), vmem(64, 8, 128), vmem(64, 8, 128),
-        vmem(*trained.shape, dtype=F32), vmem(8, 2, 4, 48, 128), vmem(8, 4, 48, 128), vmem(512, 32, dtype=F32),
+        vmem(64, 8, 128), vmem(64, 8, 128), vmem(32, 8, 128), vmem(2, FF, 256), vmem(64, 8, 128),
+        vmem(*trained.shape, dtype=F32), vmem(8, 2, 4, 48, 128), vmem(8, 4, 48, 128), vmem(2, 2, 2, 48, 128), vmem(512, 32, dtype=F32),
         vmem(2, 16, wide[0], dtype=F32), vmem(2, 16, wide[0]), vmem(2, 16, wide[0]),
-        dma(8), dma(8 + 2 * count), dma(2 * count), dma(2 * count), dma(), dma(), dma(),
-        dma(count), dma(count), dma(count), dma(count), dma(count), dma(count),
-        dma(), dma(), dma(), dma(), dma(), dma(), dma(8), dma(8), dma(2), dma(2 * count),
+        dma(10), dma(8 + 2 * count), dma(), dma(2 * count), dma(), dma(),
+        dma(count), dma(count), dma(count), dma(count),
+        dma(), dma(), dma(), dma(8), dma(), dma(), dma(2),
     ]
     scratch += [vmem(*((4, 128, wide[0]) if n == 0 else (256, wide[n]))) for n in range(count)]
     scratch += [vmem(*((2, FF, 128) if n == 0 else (128, wide[n]))) for n in range(count)]
@@ -387,9 +409,9 @@
     scratch += [vmem(8, 2 if n == 0 else 1, 16, wide[n] // 2) for n in range(count)]
     out = pl.pallas_call(
         kernel,
-        out_shape=(pltpu.VMEM(tokens.shape, BF), pltpu.VMEM(down.shape, BF)),
+        out_shape=(pltpu.VMEM((64, 8, 128), BF), pltpu.VMEM((512, 32), F32), pltpu.VMEM(down.shape, BF)),
         in_specs=[A] * 7,
-        out_specs=(V, V),
+        out_specs=(A, A, A),
         scratch_shapes=scratch,
         compiler_params=pltpu.CompilerParams(collective_id=0, has_side_effects=True),
         name="moe_step",
@@ -398,9 +420,9 @@
     return pl.pallas_call(
         write_out,
         out_shape=(jax.ShapeDtypeStruct(tokens.shape, BF), jax.ShapeDtypeStruct(down.shape, BF)),
-        in_specs=[V, V],
+        in_specs=[V, V, V],
         out_specs=(A, A),
-        scratch_shapes=[dma(2)],
+        scratch_shapes=[vmem(*tokens.shape), dma(2)],
         name="write_out",
     )(*out)
 

time: 60.5 us -> 59.2 us (0.979)
  Pallas kernels: 59.7 us -> 58.4 us
    pallas_call x1, Pallas kernels: 58.8 us -> 57.5 us  [local(): pl.pallas_call(kernel, out_shape=(pltpu.VMEM((64, 8, 128), BF), pltpu.VME...]
where the time goes in v4:
time: 59.2 us; the launch traced here: 59 us
  Pallas kernels  58.4 us (99%)
  between operations  0.64 us (1%)
    pallas_call x1, Pallas kernels, local(): pl.pallas_call(kernel, out_shape=(pltpu.VMEM((64, 8, 128), BF), pltpu.VME...  57.5 us

profile of v4, /device:TPU:1, one launch (start us, length us, event | category | flops | bytes accessed | tf_op | source)
XLA Modules:
  0.0 59.0 jit_solution(8234326905349706877)
XLA Ops:
  0.6 57.5 %moe_step.1 = (bf16[64,8,128]{2,1,0:T(8,128)(2,1)S(1)}, f32[512,32]{1,0:T(8,128)S(1)}, bf16[4,768,128]{2,1,0:T(8,128)(2,1)S(1)}) custom-call(bf16[32,128]{1,0:T(8,128)(2,1)} %refs_0_.1, s32[8,32]{1,0:T(8,128)} %bitcast.2, f32[8,32]{1,0:T(8,128)} %bitcast.3, bf16[4,128,768]{2,1,0:T(8,128)(2,1)} %refs_3_.1, bf16[4,128,768]{2,1,0:T(8,128)(2,1)} %refs_4_.1, ...), custom_call_target="tpu_custom_call" | custom-call | tf_op jit(solution)/shard_map/moe_step/pallas_call | solution.py:410
  58.1 0.9 %write_out.1 = (bf16[32,128]{1,0:T(8,128)(2,1)}, bf16[4,768,128]{2,1,0:T(8,128)(2,1)}) custom-call(bf16[64,8,128]{2,1,0:T(8,128)(2,1)S(1)} %get-tuple-element.5.ret, f32[512,32]{1,0:T(8,128)S(1)} %get-tuple-element.6.shares, bf16[4,768,128]{2,1,0:T(8,128)(2,1)S(1)} %get-tuple-element.7.synced), custom_call_target="tpu_custom_call" | custom-call | tf_op jit(solution)/shard_map/write_out/pallas_call | solution.py:420

commit v5 on v4

--- a/solution.py
+++ b/solution.py
@@ -15,7 +15,7 @@
 DIRECT = (3, 4)
 EARLY = 2
 SOON = 1
-ORDER = (0, 1, 2, 10, 11, 3, 12, 20, 4, 21, 13, 22, 40, 14, 31, 32, 23, 30, 24, 33, 34)
+ORDER = (0, 1, 2, 10, 11, 3, 12, 20, 4, 21, 13, 22, 40, 14, 31, 23, 32, 30, 24, 33, 34)
 AWAY = sorted(
     ((dy, flip) for dy in range(8) for flip in range(8) if dy or flip),
     key=lambda a: -(min(a[0], 8 - a[0]) + (a[1] >> 2) * 2 * (1 - (a[1] & 1)) + (a[1] & 1)),
@@ -44,10 +44,10 @@
     (tokens_hbm, routes_hbm, route_weight_hbm, gate, up, down, trained, ret, shares, synced,
      tokens, routes, route_weight, out_tok, arr_s, arr_o, wd, oute, td, td_send, td_relay, td_far, combine,
      half_sum, half_send, half_recv) = refs[:26]
-    (load_sem, wl_sem, sent, w_recv, d_recv, o_recv, p_recv, r_recv, h_recv, f_recv,
-     e_recv, a_recv, b_recv, x_recv, half_sem, s_sem, v_recv) = refs[26:43]
+    (load_sem, sent, w_recv, d_recv, o_recv, p_recv, r_recv, h_recv, f_recv,
+     e_recv, a_recv, b_recv, x_recv, half_sem, s_sem, v_recv) = refs[26:42]
     count = len(PIECES)
-    weights, leaving, psend, precv, pagg, hid = (refs[43 + count * i : 43 + count * (i + 1)] for i in range(6))
+    weights, leaving, psend, precv, pagg, hid = (refs[42 + count * i : 42 + count * (i + 1)] for i in range(6))
 
     z, xl, g = lax.axis_index("z"), lax.axis_index("xl"), lax.axis_index("expert")
     other = 1 - xl
@@ -96,18 +96,18 @@
                 for q in range(4):
                     pair = xl if q < 2 else other
                     loads[0].append(pltpu.make_async_copy(
-                        src.at[2 * pair + q % 2, :, cols], weights[0].at[q, :, into], wl_sem.at[4 * m + q]))
+                        src.at[2 * pair + q % 2, :, cols], weights[0].at[q, :, into], s_sem))
             else:
                 loads[n].append(pltpu.make_async_copy(
-                    src.at[2 * xl + e, :, cols], weights[n].at[0:WIDTH, into], wl_sem.at[6 + 2 * n + m]))
+                    src.at[2 * xl + e, :, cols], weights[n].at[0:WIDTH, into], s_sem))
                 staged.append(pltpu.make_async_copy(
                     src.at[2 * other + e, :, cols], leaving[n].at[:, into], s_sem))
-                sends[n].append(pltpu.make_async_remote_copy(
-                    leaving[n].at[:, into], weights[n].at[WIDTH : 2 * WIDTH, into],
-                    sent, w_recv.at[2 * n + m], **at(z, other, g)))
+        if n:
+            sends[n].append(pltpu.make_async_remote_copy(
+                leaving[n], weights[n].at[WIDTH : 2 * WIDTH], sent, w_recv.at[n + 1], **at(z, other, g)))
     down_loads, down_sends, down_staged = [], [], []
     for e in range(2):
-        down_loads.append(pltpu.make_async_copy(down.at[2 * xl + e], wd.at[e, :, 0:WIDTH], load_sem.at[4 + e]))
+        down_loads.append(pltpu.make_async_copy(down.at[2 * xl + e], wd.at[e, :, 0:WIDTH], s_sem))
         down_staged.append(pltpu.make_async_copy(down.at[2 * other + e], leaving[0].at[e], s_sem))
         down_sends.append(pltpu.make_async_remote_copy(
             leaving[0].at[e], wd.at[e, :, WIDTH : 2 * WIDTH], sent, w_recv.at[e], **at(z, other, g)))
@@ -134,7 +134,7 @@
         arr_s[2 * g] = out_tok[2 * g]
         arr_s[2 * g + 1] = out_tok[2 * g + 1]
 
-    for copy in staged + down_staged:
+    for copy in staged + sum(loads, []) + down_staged + down_loads:
         copy.wait()
     with jax.named_scope("barrier"):
         pl.semaphore_wait(barrier, 70)
@@ -184,7 +184,7 @@
             dz = 2 - 4 * way
             push(td_far.at[far, way], synced.at[pl.ds(2 * way, 2), rows_of(along(-dz) * 2 + side)], send_sem, recv_sem, dz)
 
-    for dz in ZAWAY:
+    for dz in (4, 1, 7, 2, 6, 3, 5):
         spread(td_send.at[along(dz), xl], mine, 0, sent, a_recv, dz)
     across = [
         pltpu.make_async_remote_copy(
@@ -219,8 +219,6 @@
     def partial(n):
         width, e = PIECES[n][1:]
         with jax.named_scope(f"wait_w{n}"):
-            for copy in loads[n]:
-                copy.wait()
             for copy in sends[n]:
                 copy.wait_recv()
         if n == 0:
@@ -321,7 +319,6 @@
         hop(n)
     with jax.named_scope("wait_wd"):
         for e in range(2):
-            down_loads[e].wait()
             down_sends[e].wait_recv()
     outs = [None, None]
     for n, (first, width, expert) in enumerate(PIECES):
@@ -398,7 +395,7 @@
         vmem(64, 8, 128), vmem(64, 8, 128), vmem(32, 8, 128), vmem(2, FF, 256), vmem(64, 8, 128),
         vmem(*trained.shape, dtype=F32), vmem(8, 2, 4, 48, 128), vmem(8, 4, 48, 128), vmem(2, 2, 2, 48, 128), vmem(512, 32, dtype=F32),
         vmem(2, 16, wide[0], dtype=F32), vmem(2, 16, wide[0]), vmem(2, 16, wide[0]),
-        dma(10), dma(8 + 2 * count), dma(), dma(2 * count), dma(), dma(),
+        dma(10), dma(), dma(1 + count), dma(), dma(),
         dma(count), dma(count), dma(count), dma(count),
         dma(), dma(), dma(), dma(8), dma(), dma(), dma(2),
     ]

time: 59.2 us -> 58.7 us (level)
  Pallas kernels: 58.4 us -> 57.5 us
    pallas_call x1, Pallas kernels: 57.5 us -> 56.6 us  [local(): pl.pallas_call(kernel, out_shape=(pltpu.VMEM((64, 8, 128), BF), pltpu.VME...]
where the time goes in v5:
time: 58.7 us; the launch traced here: 58.1 us
  Pallas kernels  57.5 us (98%)
  between operations  0.64 us (1%)
    pallas_call x1, Pallas kernels, local(): pl.pallas_call(kernel, out_shape=(pltpu.VMEM((64, 8, 128), BF), pltpu.VME...  56.6 us

profile of v5, /device:TPU:1, one launch (start us, length us, event | category | flops | bytes accessed | tf_op | source)
XLA Modules:
  0.0 58.1 jit_solution(15051049269035221102)
XLA Ops:
  0.6 56.6 %moe_step.1 = (bf16[64,8,128]{2,1,0:T(8,128)(2,1)S(1)}, f32[512,32]{1,0:T(8,128)S(1)}, bf16[4,768,128]{2,1,0:T(8,128)(2,1)S(1)}) custom-call(bf16[32,128]{1,0:T(8,128)(2,1)} %refs_0_.1, s32[8,32]{1,0:T(8,128)} %bitcast.2, f32[8,32]{1,0:T(8,128)} %bitcast.3, bf16[4,128,768]{2,1,0:T(8,128)(2,1)} %refs_3_.1, bf16[4,128,768]{2,1,0:T(8,128)(2,1)} %refs_4_.1, ...), custom_call_target="tpu_custom_call" | custom-call | tf_op jit(solution)/shard_map/moe_step/pallas_call | solution.py:407
  57.2 0.9 %write_out.1 = (bf16[32,128]{1,0:T(8,128)(2,1)}, bf16[4,768,128]{2,1,0:T(8,128)(2,1)}) custom-call(bf16[64,8,128]{2,1,0:T(8,128)(2,1)S(1)} %get-tuple-element.5.ret, f32[512,32]{1,0:T(8,128)S(1)} %get-tuple-element.6.shares, bf16[4,768,128]{2,1,0:T(8,128)(2,1)S(1)} %get-tuple-element.7.synced), custom_call_target="tpu_custom_call" | custom-call | tf_op jit(solution)/shard_map/write_out/pallas_call | solution.py:417
